TPU v7x, 256 devices: a whole 4x4x8 slice. The times are simulated.
256 devices in a mesh: row: 32 (over z, y), dep: 8 (over x, core).
Axes of the slice: x: 4, y: 4, z: 8, core: 2. Of those that a mesh axis runs over, the one named last changes fastest.
Arguments:
- x_vol: bfloat16 [2, 16, 512, 32, 128], P(None, 'dep', 'row')
- w_conv1: bfloat16 [3, 3, 3, 128, 128], replicated
- w_conv2: bfloat16 [3, 3, 3, 128, 128], replicated
- g_out: bfloat16 [2, 16, 512, 32, 128], P(None, 'dep', 'row')
Outputs:
- output 1: bfloat16 [2, 16, 512, 32, 128], P(None, 'dep', 'row')
- output 2: bfloat16 [2, 16, 512, 32, 128], P(None, 'dep', 'row')
- output 3: float32 [3, 3, 3, 128, 128], replicated
- output 4: float32 [3, 3, 3, 128, 128], replicated
All inputs are finite; a program needn't handle non-finite values.
Results may differ from a plain program's by a relative error of at most 0.00921345.
Values are sent between devices in bfloat16 or wider.
A program may use at most 768 MiB of HBM per device.

v0:
```python
import jax
import jax.numpy as jnp
from jax import lax
from jax.sharding import PartitionSpec as P, NamedSharding

FWD_DIMS = ('NDHWC', 'DHWIO', 'NDHWC')
TRN_DIMS = ('NDHWC', 'DHWOI', 'NDHWC')
WGT_DIMS = ('CDHWN', 'IDHWO', 'DHWNC')


def gelu_tanh(values):
    return jax.nn.gelu(values, approximate=True)


def conv_tile(volume, kernel, dims):
    return lax.conv_general_dilated(volume, kernel, (1, 1, 1), ((0, 0), (0, 0), (1, 1)), dimension_numbers=dims, preferred_element_type=jnp.float32)


def add_halo(tile_vals, axis_name, axis_count, vol_axis):
    up_pairs = [(src_pos, src_pos + 1) for src_pos in range(axis_count - 1)]
    down_pairs = [(src_pos + 1, src_pos) for src_pos in range(axis_count - 1)]
    extent = tile_vals.shape[vol_axis]
    last_face = lax.slice_in_dim(tile_vals, extent - 1, extent, axis=vol_axis)
    first_face = lax.slice_in_dim(tile_vals, 0, 1, axis=vol_axis)
    from_below = lax.ppermute(last_face, axis_name, up_pairs)
    from_above = lax.ppermute(first_face, axis_name, down_pairs)
    return jnp.concatenate([from_below, tile_vals, from_above], axis=vol_axis)


def solution(mesh):
    row_count = mesh.shape['row']
    dep_count = mesh.shape['dep']
    vol_spec = P(None, 'dep', 'row', None, None)

    def with_halo(tile_vals):
        return add_halo(add_halo(tile_vals, 'dep', dep_count, 1), 'row', row_count, 2)

    def local_step(x_tile, w_conv1, w_conv2, g_tile):
        x_ext = with_halo(x_tile)
        pre_act = conv_tile(x_ext, w_conv1, FWD_DIMS).astype(jnp.bfloat16)
        gelu_f32, gelu_back = jax.vjp(gelu_tanh, pre_act.astype(jnp.float32))
        gelu_bf = gelu_f32.astype(jnp.bfloat16)
        gelu_ext = with_halo(gelu_bf)
        y_tile = (conv_tile(gelu_ext, w_conv2, FWD_DIMS) + x_tile.astype(jnp.float32)).astype(jnp.bfloat16)
        g_ext = with_halo(g_tile)
        dgelu_f32 = conv_tile(g_ext, w_conv2[::-1, ::-1, ::-1], TRN_DIMS)
        dw_conv2 = lax.psum(conv_tile(gelu_ext, g_tile, WGT_DIMS), ('row', 'dep'))
        dpre_bf = gelu_back(dgelu_f32)[0].astype(jnp.bfloat16)
        dpre_ext = with_halo(dpre_bf)
        dx_tile = (conv_tile(dpre_ext, w_conv1[::-1, ::-1, ::-1], TRN_DIMS) + g_tile.astype(jnp.float32)).astype(jnp.bfloat16)
        dw_conv1 = lax.psum(conv_tile(x_ext, dpre_bf, WGT_DIMS), ('row', 'dep'))
        return (y_tile, dx_tile, dw_conv1, dw_conv2)

    return jax.shard_map(local_step, mesh=mesh, in_specs=(vol_spec, P(), P(), vol_spec), out_specs=(vol_spec, vol_spec, P(), P()), check_vma=False)
```

profile of v0, /device:TPU:1, one launch (start us, length us, event | category | flops | bytes accessed | tf_op | source)
XLA Modules:
  0.0 415.8 jit_solution(16337185778267415853)
XLA Ops:
  8.4 4.5 %collective-permute-start = (bf16[2,1,16,32,128]{4,3,2,1,0:T(8,128)(2,1)S(1)}, bf16[2,1,16,32,128]{4,3,2,1,0:T(8,128)(2,1)S(1)}, u32[]{:S(2)}, u32[]{:S(2)}) collective-permute-start(bf16[2,1,16,32,128]{4,3,2,1,0:T(8,128)(2,1)S(1)} %get-tuple-element.29), channel_id=1, source_target_pairs={{0,1},{1,2},{2,3},{3,4},{4,5},{5,6},{6,7},{8,9},{9,10},{10,11},{11... | collective-permute-start | bytes 786440 | tf_op jit(solution)/shard_map/ppermute | solution.py:25
  12.9 1.9 collective-permute-start.1
  15.9 3.8 collective-permute-start.8
  19.7 1.9 collective-permute-start.9
  21.9 1.3 collective-permute-start.3
  23.2 4.0 collective-permute-start.2
  27.5 1.3 collective-permute-start.11
  28.8 4.1 collective-permute-start.10
  36.1 2.1 fusion.14
  38.2 5.1 %fusion.56 = (bf16[2,16,16,5,128]{4,2,3,1,0:T(8,128)(2,1)S(1)}, bf16[2,16,16,5,128]{4,2,3,1,0:T(8,128)(2,1)S(1)}) fusion(bf16[3,3,3,128,128]{4,3,2,1,0:T(8,128)(2,1)S(1)} %copy-done, bf16[4,18,2,8,7,128]{5,2,4,3,1,0:T(2,128)(2,1)S(1)} %fusion.14, pred[16,5]{0,1:T(8,128)(4,1)S(1)} %copy-done.8), kind=kOutput, calls=%fused_computation.55 | convolution fusion | flops 2268856320 | bytes 4259920 | tf_op jit(solution)/shard_map/conv_general_dilated | solution.py:16
  43.3 1.5 copy.41
  44.8 2.7 fusion.77
  49.0 1.9 collective-permute-start.5
  51.3 4.7 %collective-permute-start.4 = (bf16[2,1,16,32,128]{4,0,3,2,1:T(2,128)(2,1)S(1)}, bf16[2,1,16,32,128]{4,0,3,2,1:T(2,128)(2,1)S(1)}, u32[]{:S(2)}, u32[]{:S(2)}) collective-permute-start(bf16[2,1,16,32,128]{4,0,3,2,1:T(2,128)(2,1)S(1)} %bitcast.117), channel_id=1, source_target_pairs={{0,1},{1,2},{2,3},{3,4},{4,5},{5,6},{6,7},{8,9},{9,10},{10,11},{11... | collective-permute-start | bytes 786440 | tf_op jit(solution)/shard_map/ppermute | solution.py:25
  59.0 1.9 fusion.15
  60.9 5.5 %fusion.52 = bf16[2,16,16,5,128]{4,2,3,1,0:T(8,128)(2,1)S(1)} fusion(bf16[2,16,16,5,128]{4,2,3,1,0:T(8,128)(2,1)S(1)} %get-tuple-element.31, bf16[3,3,3,128,128]{4,3,2,1,0:T(8,128)(2,1)S(1)} %copy-done.7, bf16[4,18,2,8,7,128]{5,2,4,3,1,0:T(2,128)(2,1)S(1)} %fusion.15, pred[16,5]{0,1:T(8,128)(4,1)S(1)} %copy-done.8), kind=kOutput, calls=%fused_computation.51 | convolution fusion | flops 2272133120 | bytes 4259920 | tf_op jit(solution)/shard_map/conv_general_dilated | solution.py:16
  66.6 1.9 collective-permute-start.13
  68.6 4.0 collective-permute-start.12
  72.7 2.9 fusion.33
  76.3 6.1 %fusion.30 = f32[3,3,3,128,128]{4,3,2,1,0:T(8,128)} fusion(bf16[4,18,16,5,128,1]{4,2,5,3,1,0:T(8,128)(2,1)S(1)} %bitcast.110, bf16[4,18,16,5,128,1]{4,2,5,3,1,0:T(8,128)(2,1)S(1)} %copy.45, bf16[4,18,16,5,128,1]{4,2,5,3,1,0:T(8,128)(2,1)S(1)} %bitcast.111, bf16[2,16,16,5,128]{4,2,3,1,0:T(8,128)(2,1)S(1)} %fusion.52, pred[16,5]{0,1:T(8,128)(4,1)S(1)} %copy-done.8), kind=kOutput, calls=%fused_computation.39 | convolution fusion | flops 2269675520 | bytes 6848592 | tf_op jit(solution)/shard_map/conv_general_dilated | solution.py:16
  83.6 1.3 collective-permute-start.7
  84.9 4.0 collective-permute-start.6
  89.2 1.3 collective-permute-start.15
  90.5 5.1 %collective-permute-start.14 = (bf16[2,4,1,32,128]{4,2,3,0,1:T(2,128)(2,1)S(1)}, bf16[2,4,1,32,128]{4,2,3,0,1:T(2,128)(2,1)S(1)}, u32[]{:S(2)}, u32[]{:S(2)}) collective-permute-start(bf16[2,4,1,32,128]{4,2,3,0,1:T(2,128)(2,1)S(1)} %get-tuple-element.14), channel_id=1, source_target_pairs={{0,8},{8,16},{16,24},{24,32},{32,40},{40,48},{48,56},{56,64},{64,7... | collective-permute-start | bytes 196616 | tf_op jit(solution)/shard_map/ppermute | solution.py:25
  95.6 3.6 fusion.90
  100.7 5.1 %fusion.44 = f32[2,16,16,5,128]{4,2,3,1,0:T(8,128)S(1)} fusion(bf16[3,3,3,128,128]{4,3,2,1,0:T(8,128)(2,1)S(1)} %copy-done.7, bf16[4,18,2,7,2,128]{5,3,2,4,1,0:T(8,128)(2,1)S(1)} %slice.92, bf16[4,18,2,8,5,128]{5,3,2,4,1,0:T(8,128)(2,1)S(1)} %copy.29, pred[16,5]{0,1:T(8,128)(4,1)S(1)} %copy-done.8), kind=kOutput, calls=%fused_computation.47 | convolution fusion | flops 2271444992 | bytes 4186192 | tf_op jit(solution)/shard_map/conv_general_dilated | solution.py:16
  112.9 10.6 %fusion.69 = f32[3,3,3,128,128]{4,3,2,1,0:T(8,128)} fusion(bf16[2,2,16,32,128]{4,3,2,1,0:T(8,128)(2,1)S(1)} %copy-done.4, bf16[2,4,1,32,128]{4,0,3,2,1:T(2,128)(2,1)S(1)} %collective-permute-done.7, bf16[2,1,16,32,128]{4,0,3,2,1:T(2,128)(2,1)S(1)} %collective-permute-done.5, bf16[2,2,16,32,128]{4,0,3,2,1:T(2,128)(2,1)S(1)} %bitcast.105, ...), kind=kOutput, calls=%fused_computation.73 | convolution fusion | flops 1780088832 | bytes 3473408 | tf_op jit(solution)/shard_map/conv_general_dilated | solution.py:16
  123.5 1.3 copy-done.2
  124.9 2.1 fusion.16
  127.1 5.1 %fusion.41 = f32[2,16,16,5,128]{4,2,3,1,0:T(8,128)S(1)} fusion(bf16[3,3,3,128,128]{4,3,2,1,0:T(8,128)(2,1)S(1)} %copy-done, bf16[4,18,2,8,7,128]{5,2,4,3,1,0:T(2,128)(2,1)S(1)} %fusion.16, pred[16,5]{0,1:T(8,128)(4,1)S(1)} %copy-done.9), kind=kOutput, calls=%fused_computation.46 | convolution fusion | flops 2265251840 | bytes 4259920 | tf_op jit(solution)/shard_map/conv_general_dilated | solution.py:16
  133.7 270.7 %all-reduce.3.cloned.1.call-done = (f32[3,3,3,128,128]{4,3,2,1,0:T(8,128)}, f32[3,3,3,128,128]{4,3,2,1,0:T(8,128)}) async-done(((f32[3,3,3,128,128]{4,3,2,1,0:T(8,128)}, f32[3,3,3,128,128]{4,3,2,1,0:T(8,128)}), (f32[3,3,3,128,128]{4,3,2,1,0:T(8,128)}, f32[3,3,3,128,128]{4,3,2,1,0:T(8,128)})) %all-reduce.3.cloned.1.call-update) | async-done | bytes 3538960 | tf_op jit(solution)/shard_map/psum | solution.py:51
  404.4 3.0 copy.100
  (94 shorter events, 24.5 us)
Async XLA Ops:
  7.2 31.0 %copy-start = (bf16[3,3,3,128,128]{4,3,2,1,0:T(8,128)(2,1)S(1)}, bf16[3,3,3,128,128]{4,3,2,1,0:T(8,128)(2,1)}, u32[]{:S(2)}) copy-start(bf16[3,3,3,128,128]{4,3,2,1,0:T(8,128)(2,1)} %param.5) | copy-start | bytes 2654212
  7.2 14.5 %copy-start.3 = (bf16[2,2,16,32,128]{4,3,2,1,0:T(8,128)(2,1)S(1)}, bf16[2,2,16,32,128]{4,3,2,1,0:T(8,128)(2,1)}, u32[]{:S(2)}) copy-start(bf16[2,2,16,32,128]{4,3,2,1,0:T(8,128)(2,1)} %param.4) | copy-start | bytes 1572868
  7.2 397.2 %all-reduce.3.cloned.1.call-start = ((), (), s32[]{:S(2)}) async-start(), calls=%async_computation | async-start | bytes 7077888 | tf_op jit(solution)/shard_map/psum | solution.py:51
  8.4 13.2 %collective-permute-start = (bf16[2,1,16,32,128]{4,3,2,1,0:T(8,128)(2,1)S(1)}, bf16[2,1,16,32,128]{4,3,2,1,0:T(8,128)(2,1)S(1)}, u32[]{:S(2)}, u32[]{:S(2)}) collective-permute-start(bf16[2,1,16,32,128]{4,3,2,1,0:T(8,128)(2,1)S(1)} %get-tuple-element.29), channel_id=1, source_target_pairs={{0,1},{1,2},{2,3},{3,4},{4,5},{5,6},{6,7},{8,9},{9,10},{10,11},{11... | collective-permute-start | bytes 786440 | tf_op jit(solution)/shard_map/ppermute | solution.py:25
  12.9 8.9 %collective-permute-start.1 = (bf16[2,1,16,32,128]{4,3,2,1,0:T(8,128)(2,1)S(1)}, bf16[2,1,16,32,128]{4,3,2,1,0:T(8,128)(2,1)S(1)}, u32[]{:S(2)}, u32[]{:S(2)}) collective-permute-start(bf16[2,1,16,32,128]{4,3,2,1,0:T(8,128)(2,1)S(1)} %get-tuple-element.28), channel_id=1, source_target_pairs={{1,0},{2,1},{3,2},{4,3},{5,4},{6,5},{7,6},{9,8},{10,9},{11,10},{12... | collective-permute-start | bytes 786440 | tf_op jit(solution)/shard_map/ppermute | solution.py:26
  15.9 11.3 %copy-start.4 = (bf16[2,2,16,32,128]{4,3,2,1,0:T(8,128)(2,1)S(1)}, bf16[2,2,16,32,128]{4,3,2,1,0:T(8,128)(2,1)}, u32[]{:S(2)}) copy-start(bf16[2,2,16,32,128]{4,3,2,1,0:T(8,128)(2,1)} %param.7) | copy-start | bytes 1572868
  15.9 11.2 %collective-permute-start.8 = (bf16[2,1,16,32,128]{4,3,2,1,0:T(8,128)(2,1)S(1)}, bf16[2,1,16,32,128]{4,3,2,1,0:T(8,128)(2,1)S(1)}, u32[]{:S(2)}, u32[]{:S(2)}) collective-permute-start(bf16[2,1,16,32,128]{4,3,2,1,0:T(8,128)(2,1)S(1)} %get-tuple-element.27), channel_id=1, source_target_pairs={{0,1},{1,2},{2,3},{3,4},{4,5},{5,6},{6,7},{8,9},{9,10},{10,11},{11... | collective-permute-start | bytes 786440 | tf_op jit(solution)/shard_map/ppermute | solution.py:25
  19.7 7.7 %collective-permute-start.9 = (bf16[2,1,16,32,128]{4,3,2,1,0:T(8,128)(2,1)S(1)}, bf16[2,1,16,32,128]{4,3,2,1,0:T(8,128)(2,1)S(1)}, u32[]{:S(2)}, u32[]{:S(2)}) collective-permute-start(bf16[2,1,16,32,128]{4,3,2,1,0:T(8,128)(2,1)S(1)} %get-tuple-element.26), channel_id=1, source_target_pairs={{1,0},{2,1},{3,2},{4,3},{5,4},{6,5},{7,6},{9,8},{10,9},{11,10},{12... | collective-permute-start | bytes 786440 | tf_op jit(solution)/shard_map/ppermute | solution.py:26
  21.9 11.1 %collective-permute-start.3 = (bf16[2,4,1,32,128]{4,3,2,1,0:T(8,128)(2,1)S(1)}, bf16[2,4,1,32,128]{4,3,2,1,0:T(8,128)(2,1)S(1)}, u32[]{:S(2)}, u32[]{:S(2)}) collective-permute-start(bf16[2,4,1,32,128]{4,3,2,1,0:T(8,128)(2,1)S(1)} %get-tuple-element.21), channel_id=1, source_target_pairs={{8,0},{16,8},{24,16},{32,24},{40,32},{48,40},{56,48},{64,56},{72,6... | collective-permute-start | bytes 196616 | tf_op jit(solution)/shard_map/ppermute | solution.py:26
  23.2 9.8 %collective-permute-start.2 = (bf16[2,4,1,32,128]{4,3,2,1,0:T(8,128)(2,1)S(1)}, bf16[2,4,1,32,128]{4,3,2,1,0:T(8,128)(2,1)S(1)}, u32[]{:S(2)}, u32[]{:S(2)}) collective-permute-start(bf16[2,4,1,32,128]{4,3,2,1,0:T(8,128)(2,1)S(1)} %get-tuple-element.20), channel_id=1, source_target_pairs={{0,8},{8,16},{16,24},{24,32},{32,40},{40,48},{48,56},{56,64},{64,7... | collective-permute-start | bytes 196616 | tf_op jit(solution)/shard_map/ppermute | solution.py:25
  27.5 28.6 %collective-permute-start.11 = (bf16[2,4,1,32,128]{4,3,2,1,0:T(8,128)(2,1)S(1)}, bf16[2,4,1,32,128]{4,3,2,1,0:T(8,128)(2,1)S(1)}, u32[]{:S(2)}, u32[]{:S(2)}) collective-permute-start(bf16[2,4,1,32,128]{4,3,2,1,0:T(8,128)(2,1)S(1)} %get-tuple-element.17), channel_id=1, source_target_pairs={{8,0},{16,8},{24,16},{32,24},{40,32},{48,40},{56,48},{64,56},{72,6... | collective-permute-start | bytes 196616 | tf_op jit(solution)/shard_map/ppermute | solution.py:26
  28.8 27.3 %collective-permute-start.10 = (bf16[2,4,1,32,128]{4,3,2,1,0:T(8,128)(2,1)S(1)}, bf16[2,4,1,32,128]{4,3,2,1,0:T(8,128)(2,1)S(1)}, u32[]{:S(2)}, u32[]{:S(2)}) collective-permute-start(bf16[2,4,1,32,128]{4,3,2,1,0:T(8,128)(2,1)S(1)} %get-tuple-element.16), channel_id=1, source_target_pairs={{0,8},{8,16},{16,24},{24,32},{32,40},{40,48},{48,56},{56,64},{64,7... | collective-permute-start | bytes 196616 | tf_op jit(solution)/shard_map/ppermute | solution.py:25
  36.0 2.1 copy-start.8
  49.0 34.4 %collective-permute-start.5 = (bf16[2,1,16,32,128]{4,0,3,2,1:T(2,128)(2,1)S(1)}, bf16[2,1,16,32,128]{4,0,3,2,1:T(2,128)(2,1)S(1)}, u32[]{:S(2)}, u32[]{:S(2)}) collective-permute-start(bf16[2,1,16,32,128]{4,0,3,2,1:T(2,128)(2,1)S(1)} %bitcast.116), channel_id=1, source_target_pairs={{1,0},{2,1},{3,2},{4,3},{5,4},{6,5},{7,6},{9,8},{10,9},{11,10},{12... | collective-permute-start | bytes 786440 | tf_op jit(solution)/shard_map/ppermute | solution.py:26
  51.3 32.1 %collective-permute-start.4 = (bf16[2,1,16,32,128]{4,0,3,2,1:T(2,128)(2,1)S(1)}, bf16[2,1,16,32,128]{4,0,3,2,1:T(2,128)(2,1)S(1)}, u32[]{:S(2)}, u32[]{:S(2)}) collective-permute-start(bf16[2,1,16,32,128]{4,0,3,2,1:T(2,128)(2,1)S(1)} %bitcast.117), channel_id=1, source_target_pairs={{0,1},{1,2},{2,3},{3,4},{4,5},{5,6},{6,7},{8,9},{9,10},{10,11},{11... | collective-permute-start | bytes 786440 | tf_op jit(solution)/shard_map/ppermute | solution.py:25
  58.9 1.9 copy-start.7
  66.6 22.3 %collective-permute-start.13 = (bf16[2,1,16,32,128]{4,2,3,0,1:T(8,128)(2,1)S(1)}, bf16[2,1,16,32,128]{4,2,3,0,1:T(8,128)(2,1)S(1)}, u32[]{:S(2)}, u32[]{:S(2)}) collective-permute-start(bf16[2,1,16,32,128]{4,2,3,0,1:T(8,128)(2,1)S(1)} %slice_bitcast_fusion.3), channel_id=1, source_target_pairs={{1,0},{2,1},{3,2},{4,3},{5,4},{6,5},{7,6},{9,8},{10,9},{11,10},{12... | collective-permute-start | bytes 786440 | tf_op jit(solution)/shard_map/ppermute | solution.py:26
  68.6 20.3 %collective-permute-start.12 = (bf16[2,1,16,32,128]{4,2,3,0,1:T(8,128)(2,1)S(1)}, bf16[2,1,16,32,128]{4,2,3,0,1:T(8,128)(2,1)S(1)}, u32[]{:S(2)}, u32[]{:S(2)}) collective-permute-start(bf16[2,1,16,32,128]{4,2,3,0,1:T(8,128)(2,1)S(1)} %slice_bitcast_fusion.4), channel_id=1, source_target_pairs={{0,1},{1,2},{2,3},{3,4},{4,5},{5,6},{6,7},{8,9},{9,10},{10,11},{11... | collective-permute-start | bytes 786440 | tf_op jit(solution)/shard_map/ppermute | solution.py:25
  83.6 12.0 %collective-permute-start.7 = (bf16[2,4,1,32,128]{4,0,3,2,1:T(2,128)(2,1)S(1)}, bf16[2,4,1,32,128]{4,0,3,2,1:T(2,128)(2,1)S(1)}, u32[]{:S(2)}, u32[]{:S(2)}) collective-permute-start(bf16[2,4,1,32,128]{4,0,3,2,1:T(2,128)(2,1)S(1)} %get-tuple-element.19), channel_id=1, source_target_pairs={{8,0},{16,8},{24,16},{32,24},{40,32},{48,40},{56,48},{64,56},{72,6... | collective-permute-start | bytes 196616 | tf_op jit(solution)/shard_map/ppermute | solution.py:26
  84.9 10.7 %collective-permute-start.6 = (bf16[2,4,1,32,128]{4,0,3,2,1:T(2,128)(2,1)S(1)}, bf16[2,4,1,32,128]{4,0,3,2,1:T(2,128)(2,1)S(1)}, u32[]{:S(2)}, u32[]{:S(2)}) collective-permute-start(bf16[2,4,1,32,128]{4,0,3,2,1:T(2,128)(2,1)S(1)} %get-tuple-element.18), channel_id=1, source_target_pairs={{0,8},{8,16},{16,24},{24,32},{32,40},{40,48},{48,56},{56,64},{64,7... | collective-permute-start | bytes 196616 | tf_op jit(solution)/shard_map/ppermute | solution.py:25
  89.2 18.1 %collective-permute-start.15 = (bf16[2,4,1,32,128]{4,2,3,0,1:T(2,128)(2,1)S(1)}, bf16[2,4,1,32,128]{4,2,3,0,1:T(2,128)(2,1)S(1)}, u32[]{:S(2)}, u32[]{:S(2)}) collective-permute-start(bf16[2,4,1,32,128]{4,2,3,0,1:T(2,128)(2,1)S(1)} %get-tuple-element.15), channel_id=1, source_target_pairs={{8,0},{16,8},{24,16},{32,24},{40,32},{48,40},{56,48},{64,56},{72,6... | collective-permute-start | bytes 196616 | tf_op jit(solution)/shard_map/ppermute | solution.py:26
  90.5 16.8 %collective-permute-start.14 = (bf16[2,4,1,32,128]{4,2,3,0,1:T(2,128)(2,1)S(1)}, bf16[2,4,1,32,128]{4,2,3,0,1:T(2,128)(2,1)S(1)}, u32[]{:S(2)}, u32[]{:S(2)}) collective-permute-start(bf16[2,4,1,32,128]{4,2,3,0,1:T(2,128)(2,1)S(1)} %get-tuple-element.14), channel_id=1, source_target_pairs={{0,8},{8,16},{16,24},{24,32},{32,40},{40,48},{48,56},{56,64},{64,7... | collective-permute-start | bytes 196616 | tf_op jit(solution)/shard_map/ppermute | solution.py:25
  110.6 1.1 copy-start.1
  123.5 1.4 copy-start.2
  123.5 1.5 copy-start.5
  124.9 2.1 copy-start.9
  404.4 3.0 copy-start.6
Sparse Core Ops, SparseCore 0:
  123.6 280.7 all-reduce.2
where the time goes:
time: 421 us; the launch traced here: 416 us
  waiting for transfers between devices  271 us (64%)
  starting transfers between devices  47.1 us (11%)
  matrix products  37.4 us (9%)
  local copies, waits for them, and re-layouts  30.6 us (7%)
  between operations  15.1 us (4%)
  other arithmetic  14.7 us (3%)
    psum x1, waiting for transfers between devices, local_step(): dw_conv1 = lax.psum(conv_tile(x_ext, dpre_bf, WGT_DIMS), ('row', 'dep'))  271 us
    conv_general_dilated x6, matrix products, conv_tile(): lax.conv_general_dilated(volume, kernel, (1, 1, 1), ((0, 0), (0, 0), (1,...  37.4 us
    ppermute x8, starting transfers between devices, add_halo(): from_below = lax.ppermute(last_face, axis_name, up_pairs)  34.2 us
    unnamed x34, local copies, waits for them, and re-layouts  13.6 us
    ppermute x8, starting transfers between devices, add_halo(): from_above = lax.ppermute(first_face, axis_name, down_pairs)  12.9 us
    concatenate x14, local copies, waits for them, and re-layouts, add_halo(): return jnp.concatenate([from_below, tile_vals, from_above], axis=vol_axis)  10.7 us
  transfers between devices with their start and end apart: 17, of which 2 were waited for; matrix products, arithmetic and copies ran while one was open for 14% of the time, Pallas kernels for 0%

commit v1 on v0

v1 whole, which is shorter than its diff:
```python
import functools

import jax
import jax.numpy as jnp
from jax import lax
from jax.experimental import pallas as pl
from jax.experimental.pallas import tpu as pltpu
from jax.sharding import PartitionSpec as P

MESH = pl.DeviceIdType.MESH
F32 = jnp.float32
BF16 = jnp.bfloat16

NB, ND, NR, NW, NC = 2, 2, 16, 32, 128
TAPS = 27
ROWS = TAPS * NC
HALF = ROWS // 2
GRP = HALF // 2
NEIGH = ((0, 1), (0, -1), (1, 0), (-1, 0), (1, 1), (1, -1), (-1, 1), (-1, -1))


def kernel(nx, ny, nz, x_hbm, w1_hbm, w2_hbm, g_hbm,
           y_hbm, dx_hbm, dw1_hbm, dw2_hbm,
           xe, ge, ze, ae, xc, gc, zc, ac,
           w1r, w2r, w1f, w2f, w1t, w2t, gp, zt, at,
           part, crecv, hsum, r1, s1, r2, s2, r3, t2, t1, th, yv, dxv,
           in_sem, hs_sem, hr_sem, cs_sem, cr_sem, as_sem, ar_sem, out_sem):
    row, dep = lax.axis_index("row"), lax.axis_index("dep")
    nrow, ndep = nz * ny, nx * 2
    zi, yi = row // ny, row % ny
    xi, ci = dep // 2, dep % 2
    other = 1 - ci

    def x_peer(k):
        return (row, ((xi + k) % nx) * 2 + ci)

    def y_peer(k):
        return (zi * ny + (yi + k) % ny, dep)

    def z_peer(k):
        return (((zi + k) % nz) * ny + yi, dep)

    core_peer = (row, xi * 2 + other)

    def halo_peer(dr, dd):
        return ((row + dr + nrow) % nrow, (dep + dd + ndep) % ndep)

    cx = pltpu.make_async_copy(x_hbm, xe.at[:, pl.ds(1, 2), pl.ds(1, NR)], in_sem.at[0])
    cg = pltpu.make_async_copy(g_hbm, ge.at[:, pl.ds(1, 2), pl.ds(1, NR)], in_sem.at[1])
    cw = [
        pltpu.make_async_copy(w2_hbm, w2r, in_sem.at[2]),
        pltpu.make_async_copy(w1_hbm, w1r, in_sem.at[3]),
        pltpu.make_async_copy(w1_hbm, w1f.at[pl.ds(0, ROWS), pl.ds(0, NC)], in_sem.at[4]),
        pltpu.make_async_copy(w1_hbm, w1f.at[pl.ds(1152, ROWS), pl.ds(NC, NC)], in_sem.at[5]),
        pltpu.make_async_copy(w2_hbm, w2f.at[pl.ds(0, ROWS), pl.ds(0, NC)], in_sem.at[6]),
        pltpu.make_async_copy(w2_hbm, w2f.at[pl.ds(1152, ROWS), pl.ds(NC, NC)], in_sem.at[7]),
    ]
    cx.start()
    cg.start()
    for c in cw:
        c.start()

    partners = [halo_peer(a, b) for a, b in NEIGH]
    partners += [x_peer(k) for k in range(1, nx)]
    partners += [y_peer(k) for k in range(1, ny)]
    partners += [z_peer(k) for k in range(1, nz)]
    barrier = pltpu.get_barrier_semaphore()
    for p in partners:
        pl.semaphore_signal(barrier, inc=1, device_id=p, device_id_type=MESH)
    pl.semaphore_wait(barrier, len(partners))

    def halo_copies(slot, ext):
        out = []
        for k, (dr, dd) in enumerate(NEIGH):
            se, de = {1: (pl.ds(2, 1), pl.ds(0, 1)), -1: (pl.ds(1, 1), pl.ds(3, 1)),
                      0: (pl.ds(1, 2), pl.ds(1, 2))}[dd]
            sr, tr = {1: (pl.ds(NR, 1), pl.ds(0, 1)), -1: (pl.ds(1, 1), pl.ds(NR + 1, 1)),
                      0: (pl.ds(1, NR), pl.ds(1, NR))}[dr]
            out.append(pltpu.make_async_remote_copy(
                src_ref=ext.at[:, se, sr], dst_ref=ext.at[:, de, tr],
                send_sem=hs_sem.at[slot, k], recv_sem=hr_sem.at[slot, k],
                device_id=halo_peer(dr, dd), device_id_type=MESH))
        return out

    hx, hg, hz, ha = (halo_copies(i, e) for i, e in enumerate((xe, ge, ze, ae)))
    pending = []

    def start(copies):
        for c in copies:
            c.start()
            pending.append(c)

    def recv(copies):
        for c in copies:
            c.wait_recv()

    cx.wait()
    start(hx)
    cg.wait()
    start(hg)

    w1f[pl.ds(ROWS, 1152), pl.ds(0, NC)] = jnp.zeros((1152, NC), BF16)
    w1f[pl.ds(0, 1152), pl.ds(NC, NC)] = jnp.zeros((1152, NC), BF16)
    w2f[pl.ds(ROWS, 1152), pl.ds(0, NC)] = jnp.zeros((1152, NC), BF16)
    w2f[pl.ds(0, 1152), pl.ds(NC, NC)] = jnp.zeros((1152, NC), BF16)
    w1t[pl.ds(ROWS, 1152), pl.ds(0, NC)] = jnp.zeros((1152, NC), BF16)
    w1t[pl.ds(0, 1152), pl.ds(NC, NC)] = jnp.zeros((1152, NC), BF16)
    w2t[pl.ds(ROWS, 1152), pl.ds(0, NC)] = jnp.zeros((1152, NC), BF16)
    w2t[pl.ds(0, 1152), pl.ds(NC, NC)] = jnp.zeros((1152, NC), BF16)
    for c in cw:
        c.wait()

    def flip(raw, out):
        for u in range(TAPS):
            block = raw[pl.ds((TAPS - 1 - u) * NC, NC), :].T
            out[pl.ds(u * NC, NC), pl.ds(0, NC)] = block
            out[pl.ds(1152 + u * NC, NC), pl.ds(NC, NC)] = block

    flip(w2r, w2t)
    flip(w1r, w1t)

    def widen(vals, store):
        v = vals.astype(F32)
        col = lax.broadcasted_iota(jnp.int32, v.shape, 1)
        left = jnp.where(col == 0, 0.0, pltpu.roll(v, 1, 1))
        right = jnp.where(col == NW - 1, 0.0, pltpu.roll(v, NW - 1, 1))
        store(0, left.astype(BF16))
        store(1, vals)
        store(2, right.astype(BF16))

    def widen_part(ext, out, b, e, r0, nr, keep):
        vals = ext[b, e, pl.ds(r0, nr)]
        if keep is not None:
            vals = jnp.where(keep, vals, jnp.zeros_like(vals))

        def store(j, piece):
            out[b, e, pl.ds(r0, nr), :, pl.ds(j * NC, NC)] = piece

        widen(vals, store)

    def widen_local(ext, out):
        for b in range(NB):
            for e in (1, 2):
                for r0 in (1, 9):
                    widen_part(ext, out, b, e, r0, 8, None)

    def both(a, b):
        return a if b is None else (b if a is None else jnp.logical_and(a, b))

    def widen_halo(ext, out):
        for b in range(NB):
            for e in range(4):
                ek = {0: dep > 0, 3: dep < ndep - 1}.get(e)
                widen_part(ext, out, b, e, 0, 1, both(ek, row > 0))
                widen_part(ext, out, b, e, NR + 1, 1, both(ek, row < nrow - 1))
                if ek is not None:
                    for r0 in (1, 9):
                        widen_part(ext, out, b, e, r0, 8, ek)

    def conv(src, wts, finish):
        for b in range(NB):
            for r0 in (0, 8):
                lhs = jnp.concatenate(
                    [src[b, e, pl.ds(r0 + dr, 8)].reshape(8 * NW, 3 * NC)
                     for e in range(4) for dr in range(3)], axis=1)
                acc = jnp.dot(lhs, wts[...], preferred_element_type=F32)
                for d in range(ND):
                    finish(b, d, r0, acc[:, d * NC:(d + 1) * NC])

    def put(ref, b, d, r0, vals):
        ref[b, d, pl.ds(r0, 8)] = vals.reshape(8, NW, NC)

    def fin_a(b, d, r0, acc):
        a = acc.astype(BF16).astype(F32)
        c0, c1 = 0.7978845608028654, 0.044715
        sq = a * a
        th_ = jnp.tanh(c0 * (a + c1 * (sq * a)))
        cdf = 0.5 * (1.0 + th_)
        z = (a * cdf).astype(BF16)
        slope = cdf + (0.5 * a) * (1.0 - th_ * th_) * (c0 * (1.0 + (3.0 * c1) * sq))
        gp[b, d, pl.ds(r0 * NW, 8 * NW)] = slope
        put(ze, b, d + 1, r0 + 1, z)
        zt[:, pl.ds((d * NB + b) * 512 + r0 * NW, 8 * NW)] = z.T

    def fin_da(b, d, r0, acc):
        da = (acc * gp[b, d, pl.ds(r0 * NW, 8 * NW)]).astype(BF16)
        put(ae, b, d + 1, r0 + 1, da)
        at[:, pl.ds((d * NB + b) * 512 + r0 * NW, 8 * NW)] = da.T

    def fin_add(base, out):
        def fin(b, d, r0, acc):
            res = base[b, d + 1, pl.ds(r0 + 1, 8)].reshape(8 * NW, NC).astype(F32)
            put(out, b, d, r0, (acc + res).astype(BF16))
        return fin

    def tap_rhs(src, u):
        ud, dr, dw = u // 9, (u // 3) % 3, u % 3
        return jnp.concatenate(
            [src[b, d + ud, pl.ds(dr, NR), :, pl.ds(dw * NC, NC)].reshape(NR * NW, NC)
             for d in range(ND) for b in range(NB)], axis=0)

    def wgrad(lhs_t, src, j, flipped):
        lhs = lhs_t[...]
        for u in range(0, TAPS, 2):
            pair = [t for t in (u, u + 1) if t < TAPS]
            rhs = jnp.concatenate([tap_rhs(src, t) for t in pair], axis=1)
            out = jnp.dot(lhs, rhs, preferred_element_type=F32)
            for n, t in enumerate(pair):
                block = out[:, n * NC:(n + 1) * NC]
                if flipped:
                    part[j, pl.ds((TAPS - 1 - t) * NC, NC), :] = block
                else:
                    part[j, pl.ds(t * NC, NC), :] = block.T

    def rcopy(src, dst, ssem, rsem, peer):
        return pltpu.make_async_remote_copy(src_ref=src, dst_ref=dst, send_sem=ssem,
                                            recv_sem=rsem, device_id=peer, device_id_type=MESH)

    def ds8(base, size):
        return pl.ds(pl.multiple_of(base, 8), size)

    def ring(g, stage):
        order = ((x_peer, xi, nx), (y_peer, yi, ny))
        return order[(g + stage) % 2]

    dws = (dw1_hbm, dw2_hbm)

    def reducer(j):
        st = {}

        def exchange(name, g, base, peers, n, src, dst):
            lst = st.setdefault(name, {}).setdefault(g, [])
            for k in range(1, n):
                lst.append(rcopy(src(k), dst(k), as_sem.at[j, g, base + k - 1],
                                 ar_sem.at[j, g, base + k - 1], peers(k)))
            start(lst)

        def core_send():
            c = rcopy(part.at[j, ds8(other * HALF, HALF)], crecv.at[j],
                      cs_sem.at[j, 0], cr_sem.at[j, 0], core_peer)
            st["core"] = c
            start([c])

        def p1():
            st["core"].wait_recv()
            for i in range(0, HALF, 216):
                hsum[j, pl.ds(i, 216)] = part[j, ds8(ci * HALF + i, 216)] + crecv[j, pl.ds(i, 216)]
            for g in range(2):
                peers, me, n = ring(g, 0)
                exchange("p1", g, 0, peers, n,
                         lambda k: hsum.at[j, ds8(g * GRP + ((me + k) % n) * 216, 216)],
                         lambda k: r1.at[j, g, k - 1])

        def p2():
            for g in range(2):
                recv(st["p1"][g])
                _, me, n = ring(g, 0)
                tot = hsum[j, ds8(g * GRP + me * 216, 216)]
                for k in range(n - 1):
                    tot = tot + r1[j, g, k]
                s1[j, g, pl.ds(0, 216)] = tot
                s1[j, g, pl.ds(216, 8)] = jnp.zeros((8, NC), F32)
                peers, me, n = ring(g, 1)
                exchange("p2", g, 3, peers, n,
                         lambda k: s1.at[j, g, ds8(((me + k) % n) * 56, 56)],
                         lambda k: r2.at[j, g, k - 1])

        def p3():
            for g in range(2):
                recv(st["p2"][g])
                _, me, n = ring(g, 1)
                tot = s1[j, g, ds8(me * 56, 56)]
                for k in range(n - 1):
                    tot = tot + r2[j, g, k]
                s2[j, g, pl.ds(0, 56)] = tot
                s2[j, g, pl.ds(56, 8)] = jnp.zeros((8, NC), F32)
                exchange("p3", g, 6, z_peer, nz,
                         lambda k: s2.at[j, g, ds8(((zi + k) % nz) * 8, 8)],
                         lambda k: r3.at[j, g, k - 1])

        def g3():
            for g in range(2):
                recv(st["p3"][g])
                tot = s2[j, g, ds8(zi * 8, 8)]
                for k in range(nz - 1):
                    tot = tot + r3[j, g, k]
                t2[j, g, ds8(zi * 8, 8)] = tot
                exchange("g3", g, 13, z_peer, nz,
                         lambda k: t2.at[j, g, ds8(zi * 8, 8)],
                         lambda k: t2.at[j, g, ds8(zi * 8, 8)])

        def g2():
            for g in range(2):
                recv(st["g3"][g])
                peers, me, n = ring(g, 1)
                t1[j, g, ds8(me * 56, 56)] = t2[j, g, pl.ds(0, 56)]
                exchange("g2", g, 20, peers, n,
                         lambda k: t2.at[j, g, pl.ds(0, 56)],
                         lambda k: t1.at[j, g, ds8(me * 56, 56)])

        def g1():
            for g in range(2):
                recv(st["g2"][g])
                peers, me, n = ring(g, 0)
                th[j, ds8(g * GRP + me * 216, 216)] = t1[j, g, pl.ds(0, 216)]
                exchange("g1", g, 23, peers, n,
                         lambda k: t1.at[j, g, pl.ds(0, 216)],
                         lambda k: th.at[j, ds8(g * GRP + me * 216, 216)])

        def core_gather():
            for g in range(2):
                recv(st["g1"][g])
            dst = dws[j].at[ds8(ci * HALF, HALF)]
            c = rcopy(th.at[j], dst, cs_sem.at[j, 1], cr_sem.at[j, 1], core_peer)
            st["last"] = c
            start([c])
            put_out(th.at[j], dst, j)

        def finish():
            st["last"].wait_recv()

        return [core_send, p1, p2, p3, g3, g2, g1, core_gather, finish]

    outs = []

    def put_out(src, dst, n):
        c = pltpu.make_async_copy(src, dst, out_sem.at[n])
        c.start()
        outs.append(c)

    red1, red2 = reducer(0), reducer(1)

    widen_local(xe, xc)
    recv(hx)
    widen_halo(xe, xc)
    conv(xc, w1f, fin_a)
    widen_local(ge, gc)
    start(hz)
    recv(hg)
    widen_halo(ge, gc)
    wgrad(zt, gc, 1, True)
    conv(gc, w2t, fin_da)
    red2[0]()
    wgrad(at, xc, 0, False)
    red2[1]()
    start(ha)
    widen_local(ze, zc)
    red1[0]()
    recv(hz)
    widen_halo(ze, zc)
    red2[2]()
    conv(zc, w2f, fin_add(xe, yv))
    red1[1]()
    red2[3]()
    put_out(yv, y_hbm, 2)
    widen_local(ae, ac)
    recv(ha)
    widen_halo(ae, ac)
    red2[4]()
    conv(ac, w1t, fin_add(ge, dxv))
    red1[2]()
    red2[5]()
    put_out(dxv, dx_hbm, 3)
    red1[3]()
    red2[6]()
    red1[4]()
    red2[7]()
    red1[5]()
    red1[6]()
    red1[7]()
    red2[8]()
    red1[8]()
    for c in outs:
        c.wait()
    for c in pending:
        c.wait_send()


def solution(mesh):
    nrow, ndep = mesh.shape['row'], mesh.shape['dep']
    ny = 4 if nrow >= 16 else 2
    nx, nz = ndep // 2, nrow // ny
    vol = P(None, 'dep', 'row', None, None)

    def local_step(x, w1, w2, g):
        ext = (NB, ND + 2, NR + 2, NW, NC)
        wide = (NB, ND + 2, NR + 2, NW, 3 * NC)
        tile = (NB, ND, NR, NW, NC)
        V = pltpu.VMEM
        DMA = pltpu.SemaphoreType.DMA
        flops = 6 * 2 * NB * ND * NR * NW * ROWS * NC
        out = pl.pallas_call(
            functools.partial(kernel, nx, ny, nz),
            out_shape=(jax.ShapeDtypeStruct(tile, BF16), jax.ShapeDtypeStruct(tile, BF16),
                       jax.ShapeDtypeStruct((ROWS, NC), F32), jax.ShapeDtypeStruct((ROWS, NC), F32)),
            in_specs=[pl.BlockSpec(memory_space=pl.ANY)] * 4,
            out_specs=(pl.BlockSpec(memory_space=pl.ANY),) * 4,
            scratch_shapes=[
                V(ext, BF16), V(ext, BF16), V(ext, BF16), V(ext, BF16),
                V(wide, BF16), V(wide, BF16), V(wide, BF16), V(wide, BF16),
                V((ROWS, NC), BF16), V((ROWS, NC), BF16),
                V((4608, 256), BF16), V((4608, 256), BF16), V((4608, 256), BF16), V((4608, 256), BF16),
                V((NB, ND, NR * NW, NC), F32),
                V((NC, 2048), BF16), V((NC, 2048), BF16),
                V((2, ROWS, NC), F32), V((2, HALF, NC), F32), V((2, HALF, NC), F32),
                V((2, 2, 3, 216, NC), F32), V((2, 2, 224, NC), F32),
                V((2, 2, 3, 56, NC), F32), V((2, 2, 64, NC), F32),
                V((2, 2, 7, 8, NC), F32), V((2, 2, 64, NC), F32),
                V((2, 2, 224, NC), F32), V((2, HALF, NC), F32),
                V(tile, BF16), V(tile, BF16),
                DMA((8,)), DMA((4, 8)), DMA((4, 8)), DMA((2, 2)), DMA((2, 2)),
                DMA((2, 2, 26)), DMA((2, 2, 26)), DMA((4,)),
            ],
            compiler_params=pltpu.CompilerParams(
                collective_id=0, has_side_effects=True, vmem_limit_bytes=67043328),
            cost_estimate=pl.CostEstimate(flops=flops, bytes_accessed=8 << 20, transcendentals=0),
            name="resblock",
        )(x, w1.reshape(ROWS, NC), w2.reshape(ROWS, NC), g)
        y, dx, dw1, dw2 = out
        return y, dx, dw1.reshape(w1.shape), dw2.reshape(w2.shape)

    return jax.shard_map(local_step, mesh=mesh, in_specs=(vol, P(), P(), vol),
                         out_specs=(vol, vol, P(), P()), check_vma=False)
```

time: 421 us -> 84.6 us (0.20); the launches traced: 416 us -> 84.4 us
  waiting for transfers between devices: 271 us -> 0 us
  Pallas kernels: 0 us -> 76.6 us
  starting transfers between devices: 47.1 us -> 0 us
  matrix products: 37.4 us -> 0 us
  local copies, waits for them, and re-layouts: 30.6 us -> 7.19 us
  other arithmetic: 14.7 us -> 0 us
  between operations: 15.1 us -> 0.65 us
    psum x1 -> x0, waiting for transfers between devices: 271 us -> none  [local_step(): dw_conv1 = lax.psum(conv_tile(x_ext, dpre_bf, WGT_DIMS), ('row', 'dep'))]
    pallas_call x0 -> x1, Pallas kernels: none -> 76.6 us  [local_step(): pl.pallas_call(functools.partial(kernel, nx, ny, nz), out_shape=(jax.Shap...]
    ppermute x16 -> x0, starting transfers between devices: 47.1 us -> none  [the longest x8 34.2 us: add_halo(): from_below = lax.ppermute(last_face, axis_name, up_pairs)]
    conv_general_dilated x6 -> x0, matrix products: 37.4 us -> none  [conv_tile(): lax.conv_general_dilated(volume, kernel, (1, 1, 1), ((0, 0), (0, 0), (1,...]
    concatenate x14 -> x0, local copies, waits for them, and re-layouts: 10.7 us -> none  [add_halo(): return jnp.concatenate([from_below, tile_vals, from_above], axis=vol_axis)]
    concatenate x5 -> x0, other arithmetic: 7.63 us -> none  [add_halo(): return jnp.concatenate([from_below, tile_vals, from_above], axis=vol_axis)]
    unnamed x34 -> x8, local copies, waits for them, and re-layouts: 13.6 us -> 7.19 us
    conv_general_dilated x3 -> x0, other arithmetic: 6.08 us -> none  [conv_tile(): lax.conv_general_dilated(volume, kernel, (1, 1, 1), ((0, 0), (0, 0), (1,...]
  transfers between devices with their start and end apart: 17 -> 0, of which waited for: 2 -> 0; matrix products, arithmetic and copies ran while one was open for 14% -> 0% of each run, Pallas kernels for 0% -> 0%
where the time goes in v1:
time: 84.6 us; the launch traced here: 84.4 us
  Pallas kernels  76.6 us (91%)
  local copies, waits for them, and re-layouts  7.19 us (8%)
    pallas_call x1, Pallas kernels, local_step(): pl.pallas_call(functools.partial(kernel, nx, ny, nz), out_shape=(jax.Shap...  76.6 us
    unnamed x8, local copies, waits for them, and re-layouts  7.19 us

profile of v1, /device:TPU:1, one launch (start us, length us, event | category | flops | bytes accessed | tf_op | source)
XLA Modules:
  0.0 84.4 jit_solution(13560188587344178980)
XLA Ops:
  0.6 76.6 %resblock.1 = (bf16[2,2,16,32,128]{4,3,2,1,0:T(8,128)(2,1)}, bf16[2,2,16,32,128]{4,3,2,1,0:T(8,128)(2,1)}, f32[3456,128]{1,0:T(8,128)}, f32[3456,128]{1,0:T(8,128)}) custom-call(bf16[2,2,16,32,128]{4,3,2,1,0:T(8,128)(2,1)} %x_hbm.1, bf16[3456,128]{1,0:T(8,128)(2,1)} %bitcast.6, bf16[3456,128]{1,0:T(8,128)(2,1)} %bitcast.7, bf16[2,2,16,32,128]{4,3,2,1,0:T(8,128)(2,1)} %g_hbm.1), custom_call_target="tpu_custom_call" | custom-call | flops 10871635968 | bytes 8388608 | tf_op jit(solution)/shard_map/resblock/pallas_call | solution.py:392
  77.2 0.0 copy-start.1
  77.2 2.0 %copy.12 = bf16[2,2,16,32,128]{4,3,2,1,0:T(8,128)(2,1)} copy(bf16[2,2,16,32,128]{4,3,2,1,0:T(8,128)(2,1)} %get-tuple-element.16) | data formatting | bytes 1048576
  79.2 1.9 %copy.13 = bf16[2,2,16,32,128]{4,3,2,1,0:T(8,128)(2,1)} copy(bf16[2,2,16,32,128]{4,3,2,1,0:T(8,128)(2,1)} %get-tuple-element.17) | data formatting | bytes 1048576
  81.1 0.0 copy-done.1
  81.1 0.0 copy-start
  81.1 1.2 %copy.14 = f32[3,3,3,128,128]{4,3,2,1,0:T(8,128)} copy(f32[3,3,3,128,128]{4,3,2,1,0:T(8,128)S(1)} %bitcast.5) | data formatting | bytes 3538944
  82.3 0.9 %copy-done = f32[3456,128]{1,0:T(8,128)S(1)} copy-done((f32[3456,128]{1,0:T(8,128)S(1)}, f32[3456,128]{1,0:T(8,128)}, u32[]{:S(2)}) %copy-start) | copy-done | bytes 1769496
  83.2 1.2 %copy.15 = f32[3,3,3,128,128]{4,3,2,1,0:T(8,128)} copy(f32[3,3,3,128,128]{4,3,2,1,0:T(8,128)S(1)} %bitcast.4) | data formatting | bytes 3538944
Async XLA Ops:
  77.2 3.9 %copy-start.1 = (f32[3456,128]{1,0:T(8,128)S(1)}, f32[3456,128]{1,0:T(8,128)}, u32[]{:S(2)}) copy-start(f32[3456,128]{1,0:T(8,128)} %get-tuple-element.10) | copy-start | bytes 5308420
  81.1 2.1 %copy-start = (f32[3456,128]{1,0:T(8,128)S(1)}, f32[3456,128]{1,0:T(8,128)}, u32[]{:S(2)}) copy-start(f32[3456,128]{1,0:T(8,128)} %get-tuple-element.11) | copy-start | bytes 5308420

commit v2 on v0

v2 whole, which is shorter than its diff:
```python
import functools

import jax
import jax.numpy as jnp
from jax import lax
from jax.experimental import pallas as pl
from jax.experimental.pallas import tpu as pltpu
from jax.sharding import PartitionSpec as P

MESH = pl.DeviceIdType.MESH
F32 = jnp.float32
BF16 = jnp.bfloat16

NB, ND, NR, NW, NC = 2, 2, 16, 32, 128
TAPS = 27
ROWS = TAPS * NC
PADDED = TAPS + 1
FIRST = (0, 10, 20)
COUNT = (10, 10, 8)
RINGS = (4, 4, 8)
ZP = 16
BASE = tuple(t * NC for t in FIRST)
OWN = tuple(t * NC for t in COUNT)
PIECE = tuple(n // r for n, r in zip(OWN, RINGS))
SUB = tuple(n // 4 for n in PIECE)
DIRS = (0, 1)
SLOTS = 4
PLANE = 9 * NC
TRIPLE = 3 * NC
CHUNKS = ((0, 0), (0, 8), (1, 0), (1, 8))
NEIGH = ((1, 0), (-1, 0), (0, 1), (0, -1), (1, 1), (1, -1), (-1, 1), (-1, -1))


def top(n):
    return pl.ds(0, n)


def inner(n):
    return pl.ds(1, n)


def others(n):
    return range(1, n)


def kernel(nx, ny, nz, x_hbm, w1_hbm, w2_hbm, g_hbm,
           y_out, dx_out, dw_out,
           xe, ge, ze, ae, xc, gc, zc, ac,
           w1r, w2r, w1f, w2f, w1t, w2t, v1f, v2f, v1t, v2t, gp, zt, at,
           acc1, acc2, part, crecv, hsum, r1, rz, r2, r15, r3, s1, s2, t2,
           in_sem, hs_sem, hr_sem, cs_sem, cr_sem, as_sem, ar_sem, greet_sem):
    row, dep = lax.axis_index("row"), lax.axis_index("dep")
    nrow, ndep = nz * ny, nx * 2
    zi, yi = row // ny, row % ny
    xi, ci = dep // 2, dep % 2

    def x_peer(k):
        return (row, ((xi + k) % nx) * 2 + ci)

    def y_peer(k):
        return (zi * ny + (yi + k) % ny, dep)

    def z_peer(k):
        return (((zi + k) % nz) * ny + yi, dep)

    core_peer = (row, xi * 2 + 1 - ci)

    def halo_peer(dr, dd):
        return ((row + dr + nrow) % nrow, (dep + dd + ndep) % ndep)

    cx = pltpu.make_async_copy(x_hbm, xe.at[:, inner(2), inner(NR)], in_sem.at[0])
    cg = pltpu.make_async_copy(g_hbm, ge.at[:, inner(2), inner(NR)], in_sem.at[1])
    cx.start()
    cg.start()

    def scope(name):
        return jax.named_scope(name)

    around = [peer(k) for peer, n in ((x_peer, nx), (y_peer, ny), (z_peer, nz)) for k in (1, n - 1)]
    partners = [halo_peer(a, b) for a, b in NEIGH] + around
    barrier = pltpu.get_barrier_semaphore()

    def signal(sem, peers):
        for p in peers:
            pl.semaphore_signal(sem, inc=1, device_id=p, device_id_type=MESH)

    signal(barrier, partners)
    cw = []

    def fetch(src, dst):
        c = pltpu.make_async_copy(src, dst, in_sem.at[2 + len(cw)])
        c.start()
        cw.append(c)

    lanes = (top(NC), pl.ds(NC, NC))

    def fetch_own(w, full):
        for d in DIRS:
            fetch(w.at[pl.ds((1 - d) * PLANE, 2 * PLANE)], full.at[:, lanes[d]])

    def fetch_edge(w, edge):
        for p in DIRS:
            for r in DIRS:
                fetch(w.at[pl.ds(2 * p * PLANE, PLANE)], edge.at[p, pl.ds(r * TRIPLE, PLANE), lanes[r]])

    fetch_own(w1_hbm, w1f)
    fetch(w2_hbm, w2r)
    with scope("barrier"):
        pl.semaphore_wait(barrier, len(partners))

    def greet(i):
        if i:
            pl.semaphore_wait(greet_sem.at[i - 1], len(around))
        if i < 3:
            signal(greet_sem.at[i], around)

    def halo_copies(slot, ext):
        out = []
        for k, (dr, dd) in enumerate(NEIGH):
            se, de = {1: (pl.ds(2, 1), top(1)), -1: (inner(1), pl.ds(3, 1)),
                      0: (inner(2), inner(2))}[dd]
            sr, tr = {1: (pl.ds(NR, 1), top(1)), -1: (inner(1), pl.ds(NR + 1, 1)),
                      0: (inner(NR), inner(NR))}[dr]
            out.append(pltpu.make_async_remote_copy(
                src_ref=ext.at[:, se, sr], dst_ref=ext.at[:, de, tr],
                send_sem=hs_sem.at[slot, min(k // 2, 1)], recv_sem=hr_sem.at[slot, min(k // 2, 1)],
                device_id=halo_peer(dr, dd), device_id_type=MESH))
        return out

    hx, hg, hz, ha = (halo_copies(i, e) for i, e in enumerate((xe, ge, ze, ae)))
    pending = []

    def start(copies):
        for c in copies:
            c.start()

    def drain(sem, region):
        pltpu.make_async_copy(region, region, sem).wait()

    def sent(sem, region):
        pending.append((sem, region))

    def start_halo(slot, ext, copies):
        start(copies)
        sent(hs_sem.at[slot, 0], ext.at[:, top(2), top(2)])
        sent(hs_sem.at[slot, 1], ext.at[:, top(2)])

    def recv_rows(slot, ext):
        drain(hr_sem.at[slot, 0], ext.at[:, top(2), top(2)])

    def recv_planes(slot, ext):
        drain(hr_sem.at[slot, 1], ext.at[:, top(2)])

    cx.wait()
    start_halo(0, xe, hx)
    cg.wait()
    start_halo(1, ge, hg)

    greet(0)
    fetch_edge(w1_hbm, v1f)
    soon = len(cw)
    fetch(w1_hbm, w1r)
    fetch_own(w2_hbm, w2f)
    fetch_edge(w2_hbm, v2f)

    blank = jnp.zeros((TRIPLE, NC), BF16)
    for edge in (v1f, v2f, v1t, v2t):
        for p in DIRS:
            for r in DIRS:
                edge[p, pl.ds((1 - r) * PLANE, TRIPLE), lanes[r]] = blank
    for j in range(2):
        part[j, pl.ds(ROWS, NC)] = jnp.zeros((NC, NC), F32)
    for c in cw[:3]:
        c.wait()

    def flip(raw, out, edge):
        for u in range(TAPS):
            block = raw[pl.ds((TAPS - 1 - u) * NC, NC), :].T
            plane, at_row = u // 9, (u % 9) * NC
            for d in DIRS:
                if plane >= 1 - d and plane <= 2 - d:
                    out[pl.ds((plane - 1 + d) * PLANE + at_row, NC), lanes[d]] = block
            if plane != 1:
                for r in DIRS:
                    edge[plane // 2, pl.ds(r * TRIPLE + at_row, NC), lanes[r]] = block

    flip(w2r, w2t, v2t)

    def widen(vals, store):
        v = vals.astype(F32)
        col = lax.broadcasted_iota(jnp.int32, v.shape, 1)
        left = jnp.where(col == 0, 0.0, pltpu.roll(v, 1, 1))
        right = jnp.where(col == NW - 1, 0.0, pltpu.roll(v, NW - 1, 1))
        store(0, left.astype(BF16))
        store(1, vals)
        store(2, right.astype(BF16))

    def widen_part(ext, out, b, e, r0, nr, keep):
        vals = ext[b, e, pl.ds(r0, nr)]
        if keep is not None:
            vals = jnp.where(keep, vals, jnp.zeros_like(vals))

        def store(j, piece):
            out[b, e, pl.ds(r0, nr), :, pl.ds(j * NC, NC)] = piece

        widen(vals, store)

    def widen_local(ext, out):
        for b in range(NB):
            for e in (1, 2):
                for r0 in (1, 9):
                    widen_part(ext, out, b, e, r0, 8, None)

    edges = ((0, row > 0), (NR + 1, row < nrow - 1))

    def widen_rows(ext, out):
        for b in range(NB):
            for e in (1, 2):
                for r0, keep in edges:
                    widen_part(ext, out, b, e, r0, 1, keep)

    def widen_planes(ext, out):
        for b in range(NB):
            for e, ek in ((0, dep > 0), (3, dep < ndep - 1)):
                for r0, keep in edges:
                    widen_part(ext, out, b, e, r0, 1, jnp.logical_and(ek, keep))
                for r0 in (1, 9):
                    widen_part(ext, out, b, e, r0, 8, ek)

    def conv_own(src, wts, acc):
        for i, (b, r0) in enumerate(CHUNKS):
            acc[i] = conv_part(src, wts, range(3), r0, b)

    def conv_part(src, wts, drs, r0, b):
        lhs = jnp.concatenate([src[b, e, pl.ds(r0 + dr, 8)].reshape(8 * NW, 3 * NC)
                               for e in (1, 2) for dr in drs], axis=1)
        rhs = jnp.concatenate([wts[pl.ds(e * PLANE + dr * TRIPLE, TRIPLE), :]
                               for e in DIRS for dr in drs], axis=0)
        return jnp.dot(lhs, rhs, preferred_element_type=F32)

    def conv_mid(src, wts, acc):
        for i, (b, r0) in enumerate(CHUNKS):
            acc[i] = conv_part(src, wts, (1,), r0, b)

    def conv_sides(src, wts, acc):
        for i, (b, r0) in enumerate(CHUNKS):
            acc[i] = acc[i] + conv_part(src, wts, (0, 2), r0, b)

    def conv_rest(src, edge, acc, finish):
        for b in range(NB):
            for d in range(ND):
                lhs = jnp.concatenate(
                    [jnp.concatenate([src[b, 3 * d, 2 * i + k] for i in range(NR // 2)], axis=0)
                     for k in range(4)], axis=1)
                pairs = jnp.dot(lhs, edge[d], preferred_element_type=F32)
                for h in range(2):
                    some = pairs[h * NC:(h + 1) * NC]
                    rows = jnp.concatenate([some[:, r * NC:(r + 1) * NC].reshape(4, 1, NW, NC)
                                            for r in DIRS], axis=1).reshape(8 * NW, NC)
                    finish(b, d, 8 * h, acc[2 * b + h, :, lanes[d]] + rows)

    def put(ref, b, d, r0, vals):
        ref[b, d, pl.ds(r0, 8)] = vals.reshape(8, NW, NC)

    def fin_a(b, d, r0, acc):
        a = acc.astype(BF16).astype(F32)
        c0, c1 = 0.7978845608028654, 0.044715
        sq = a * a
        th_ = jnp.tanh(c0 * (a + c1 * (sq * a)))
        cdf = 0.5 * (1.0 + th_)
        z = (a * cdf).astype(BF16)
        slope = cdf + (0.5 * a) * (1.0 - th_ * th_) * (c0 * (1.0 + (3.0 * c1) * sq))
        gp[b, d, pl.ds(r0 * NW, 8 * NW)] = slope
        put(ze, b, d + 1, r0 + 1, z)
        zt[:, pl.ds((d * NB + b) * 512 + r0 * NW, 8 * NW)] = z.T

    def fin_da(b, d, r0, acc):
        da = (acc * gp[b, d, pl.ds(r0 * NW, 8 * NW)]).astype(BF16)
        put(ae, b, d + 1, r0 + 1, da)
        at[:, pl.ds((d * NB + b) * 512 + r0 * NW, 8 * NW)] = da.T

    def fin_add(base, out):
        def fin(b, d, r0, acc):
            res = base[b, d + 1, pl.ds(r0 + 1, 8)].reshape(8 * NW, NC).astype(F32)
            out[pl.ds((b * ND + d) * 512 + r0 * NW, 8 * NW), :] = (acc + res).astype(BF16)
        return fin

    def tap_rhs(src, u):
        ud, dr, dw = u // 9, (u // 3) % 3, u % 3
        return jnp.concatenate(
            [src[b, d + ud, pl.ds(dr, NR), :, pl.ds(dw * NC, NC)].reshape(NR * NW, NC)
             for d in range(ND) for b in range(NB)], axis=0)

    def wgrad(lhs_t, src, j, g, flipped):
        lhs = lhs_t[...]
        taps = [t for t in range(FIRST[g], FIRST[g] + COUNT[g]) if t < TAPS]
        for n in range(0, len(taps), 2):
            pair = taps[n:n + 2]
            rhs = jnp.concatenate(
                [tap_rhs(src, TAPS - 1 - t if flipped else t) for t in pair], axis=1)
            out = jnp.dot(lhs, rhs, preferred_element_type=F32)
            for m, t in enumerate(pair):
                block = out[:, m * NC:(m + 1) * NC]
                part[j, pl.ds(t * NC, NC), :] = block if flipped else block.T

    def rcopy(src, dst, ssem, rsem, peer):
        return pltpu.make_async_remote_copy(src_ref=src, dst_ref=dst, send_sem=ssem,
                                            recv_sem=rsem, device_id=peer, device_id_type=MESH)

    def ds8(base, size):
        return pl.ds(pl.multiple_of(base, 8), size)

    rings = ((x_peer, xi), (y_peer, yi), (z_peer, zi))

    def reducer(n, j, g):
        own, piece, sub, n1 = OWN[g], PIECE[g], SUB[g], RINGS[g]
        half = piece // 2
        base = BASE[g]
        dw_mine = dw_out.at[j]
        (peer1, me1), (peer2, me2) = rings[g], rings[(1, 0, 0)[g]]
        sides = (peer1(1), peer1(n1 - 1))
        everything = crecv.at[n, top(own)]
        got2, got3, got15 = r2.at[n], r3.at[n], r15.at[n]

        def sems(phase, i):
            return as_sem.at[n, phase], ar_sem.at[n, i]

        def arrived(i, region):
            drain(ar_sem.at[n, i], region)

        def exchange(phase, i, peers, n, src, dst):
            start([rcopy(src(k), dst(k), *sems(phase, i), peers(k)) for k in others(n)])

        def core_send():
            start([rcopy(part.at[j, pl.ds(base, own)], everything,
                         cs_sem.at[n, 0], cr_sem.at[n, 0], core_peer)])

        def rows_of(k, h):
            return ds8(((me1 + k) % n1) * piece + h * half, half)

        def rows_at(k):
            return ds8(((me1 + k) % n1) * piece, piece)

        def from_core():
            drain(cr_sem.at[n, 0], everything)
            for i in range(0, own, piece):
                hsum[n, pl.ds(i, piece)] = part[j, pl.ds(base + i, piece)] + crecv[n, pl.ds(i, piece)]

        def absorb(rows, more):
            hsum[n, rows] = hsum[n, rows] + more

        def ring_copy(i):
            k, h = ((2, 0), (2, 1), (1, 1), (3, 0), (1, 0), (3, 1))[i]
            return rcopy(hsum.at[n, rows_of(k, h)], r1.at[n, i],
                         *sems(0, min(i, 2)), sides[i % 2])

        def p1():
            from_core()
            start([ring_copy(i) for i in range(4)])

        def p1m():
            for i, k in enumerate((1, 3)):
                arrived(i, r1.at[n, i])
                absorb(rows_of(k, i), r1[n, i])
                start([ring_copy(4 + i)])

        def flow(d, s):
            return (4 - s) if d == 0 else (4 + s)

        def z_copy(d, s, src, part_rows):
            start([rcopy(hsum.at[n, src], rz.at[n, d, s, part_rows], *sems(0, 4 * d + s), sides[d])])

        def part_of(h):
            return pl.ds(h * half, half)

        def z0():
            from_core()
            for d in DIRS:
                z_copy(d, 0, rows_of(4, d), part_of(d))
            for d in DIRS:
                z_copy(d, 1, rows_of(flow(d, 1), 1 - d), part_of(1 - d))

        def z1():
            for d in DIRS:
                arrived(4 * d, rz.at[n, d, 0, part_of(d)])
                rows = rows_of(flow(d, 1), d)
                absorb(rows, rz[n, d, 0, part_of(d)])
                z_copy(d, 1, rows, part_of(d))

        def z_step(s):
            def step():
                for d in DIRS:
                    arrived(4 * d + s - 1, rz.at[n, d, s - 1])
                    rows = rows_at(flow(d, s))
                    absorb(rows, rz[n, d, s - 1])
                    z_copy(d, s, rows, top(piece))
            return step

        def plane(phase, i, src, dst):
            for kx in range(4):
                for ky in range(4):
                    k = 4 * kx + ky
                    if k:
                        px, py = (xi + kx) % nx, (yi + ky) % nx
                        start([rcopy(src(px * 4 + py), dst(k - 1), *sems(phase, i),
                                     (zi * ny + py, px * 2 + ci))])

        def z_end():
            for d in DIRS:
                arrived(4 * d + 3, rz.at[n, d, 3])
            s1[n, top(piece)] = hsum[n, rows_at(0)] + rz[n, 0, 3] + rz[n, 1, 3]
            plane(1, 8, lambda q: s1.at[n, ds8(q * 8, 8)], lambda k: r15.at[n, k])

        def z_spread():
            arrived(8, got15)
            q = (xi * 4 + yi) * 8
            tot = s1[n, ds8(q, 8)]
            for k in range(15):
                tot = tot + r15[n, k]
            t2[n, top(8)] = tot
            rows = ds8(base + me1 * piece + q, 8)
            plane(2, 9, lambda q: t2.at[n, top(8)], lambda k: dw_mine.at[rows])
            dw_out[j, rows] = tot

        def p2():
            arrived(2, r1.at[n, pl.ds(2, 4)])
            for h, (u, v) in enumerate(((3, 4), (2, 5))):
                s1[n, part_of(h)] = hsum[n, rows_of(0, h)] + r1[n, u] + r1[n, v]
            exchange(1, 8, peer2, 4, lambda k: s1.at[n, ds8(((me2 + k) % nx) * sub, sub)],
                     lambda k: r2.at[n, k - 1])

        def p3():
            arrived(8, got2)
            tot = s1[n, ds8(me2 * sub, sub)]
            for k in range(3):
                tot = tot + r2[n, k]
            s2[n, top(sub)] = tot
            s2[n, pl.ds(sub, nz * ZP - sub)] = jnp.zeros((nz * ZP - sub, NC), F32)
            exchange(2, 9, z_peer, nz, lambda k: s2.at[n, ds8(((zi + k) % nz) * ZP, ZP)],
                     lambda k: r3.at[n, k - 1])

        def g3():
            arrived(9, got3)
            mine = ds8(zi * ZP, ZP)
            tot = s2[n, mine]
            for k in range(nz - 1):
                tot = tot + r3[n, k]
            t2[n, mine] = tot
            exchange(3, 10, z_peer, nz, lambda k: t2.at[n, mine], lambda k: t2.at[n, mine])

        def out_rows(k, h=0, size=piece):
            return ds8(base + ((me1 + k) % n1) * piece + h * half, size)

        def pass_on(rows, i, d):
            start([rcopy(dw_mine.at[rows], dw_mine.at[rows], *sems(3 if g == 2 else 5, i), sides[d])])

        def to_core(rows):
            start([rcopy(dw_mine.at[rows], dw_mine.at[rows], cs_sem.at[n, 1], cr_sem.at[n, 1], core_peer)])

        def g2():
            arrived(10, got3)
            rows = ds8(base + me1 * piece + me2 * sub, sub)
            exchange(4, 11, peer2, 4, lambda k: t2.at[n, top(sub)], lambda k: dw_mine.at[rows])
            dw_out[j, rows] = t2[n, top(sub)]

        def g1():
            arrived(11, got2)
            for i in range(4):
                pass_on(out_rows(0, (i + i // 2) % 2, half), 12 + min(i, 2), i % 2)
            to_core(out_rows(0))

        def g1m():
            for d, k in enumerate((3, 1)):
                rows = out_rows(k, d, half)
                arrived(12 + d, dw_mine.at[rows])
                pass_on(rows, 14, d)
                to_core(rows)

        def gather_end():
            arrived(14, r1.at[n, pl.ds(2, 4)])
            for k, h in ((3, 1), (1, 0)):
                to_core(out_rows(k, h, half))
            to_core(out_rows(2))

        def w0():
            arrived(9, got15)
            for d in DIRS:
                pass_on(out_rows(0), 12 + 4 * d, d)
            to_core(out_rows(0))

        def w_step(s):
            def step():
                for d in DIRS:
                    k = 8 - s if d == 0 else s
                    whole = out_rows(k)
                    arrived(12 + 4 * d + s - 1, dw_mine.at[whole])
                    pass_on(whole if s < 3 else out_rows(k, d, half), 12 + 4 * d + s, d)
                    to_core(whole)
            return step

        def w_end():
            for d in DIRS:
                arrived(15 + 4 * d, dw_mine.at[out_rows(4, d, half)])
            to_core(out_rows(4))

        def sent_all():
            ring_bytes = crecv.at[n, top((n1 - 1) * piece)]
            middle = (got15, got15) if g == 2 else (got2, got3, got3, got2)
            for i, region in enumerate((ring_bytes,) + middle + (ring_bytes,)):
                drain(as_sem.at[n, i], region)
            drain(cs_sem.at[n, 1], everything)

        def finish():
            drain(cr_sem.at[n, 1], everything)
            drain(cs_sem.at[n, 0], everything)

        steps = dict(cs=core_send, fin=finish, end=sent_all)
        if g == 2:
            steps.update(p1=z0, z1=z1, z2=z_step(2), z3=z_step(3), p2=z_end, p3=z_spread, g1=w0, w1=w_step(1),
                         w2=w_step(2), w3=w_step(3), gc=w_end)
        else:
            steps.update(p1=p1, p1m=p1m, p2=p2, p3=p3, g3=g3, g2=g2, g1=g1, g1m=g1m, gc=gather_end)
        return steps

    table = {}
    for i, c in enumerate("ABYabz"):
        g = i % 3
        table[c] = (g + (c == "Y"), int(c.isupper()), g, int(c not in "AB"))
    chains = {name: reducer(*spec[:3]) for name, spec in table.items()}

    def sums(*words):
        for word in words:
            names, step = word.split(".")
            for c in names:
                with scope(c + "_" + step):
                    chains[c][step]()

    def on_core(core, *words):
        @pl.when(ci == core)
        def _():
            sums(*words)

    def give(c):
        on_core(1 - table[c][3], c + ".cs")

    with scope("xlocal"):
        widen_local(xe, xc)
        conv_mid(xc, w1f, acc1)
    with scope("glocal"):
        widen_local(ge, gc)
        conv_mid(gc, w2t, acc2)
    greet(1)
    with scope("xrows"):
        recv_rows(0, xe)
    with scope("c1own"):
        widen_rows(xe, xc)
        conv_sides(xc, w1f, acc1)
    with scope("grows"):
        recv_rows(1, ge)
    with scope("ct2own"):
        widen_rows(ge, gc)
        conv_sides(gc, w2t, acc2)
    greet(2)
    for c in cw[3:soon]:
        c.wait()
    with scope("xplanes"):
        recv_planes(0, xe)
    with scope("c1rest"):
        widen_planes(xe, xc)
        conv_rest(xc, v1f, acc1, fin_a)
    greet(3)
    with scope("gplanes"):
        recv_planes(1, ge)
    with scope("gplanesw"):
        widen_planes(ge, gc)
    start_halo(2, ze, hz)
    for c in "YBA":
        with scope("d2"):
            wgrad(zt, gc, 1, table[c][2], True)
        give(c)
    with scope("ct2rest"):
        conv_rest(gc, v2t, acc2, fin_da)
    start_halo(3, ae, ha)
    on_core(0, "B.p1")
    on_core(1, "Y.p1")
    with scope("d1z"):
        wgrad(at, xc, 0, 2, False)
    give("z")
    on_core(0, "A.p1")
    with scope("d1b"):
        wgrad(at, xc, 0, 1, False)
    give("b")
    with scope("d1a"):
        wgrad(at, xc, 0, 0, False)
    give("a")
    on_core(1, "Y.z1")
    with scope("late"):
        for c in cw[soon:]:
            c.wait()
        flip(w1r, w1t, v1t)
    with scope("zhalo"):
        widen_local(ze, zc)
        recv_rows(2, ze)
        widen_rows(ze, zc)
    on_core(1, "z.p1")
    with scope("c2own"):
        conv_own(zc, w2f, acc1)
    on_core(0, "B.p1m", "A.p1m")
    on_core(1, "b.p1")
    with scope("zplanes"):
        recv_planes(2, ze)
        widen_planes(ze, zc)
    on_core(1, "a.p1", "Y.z2")
    with scope("c2rest"):
        conv_rest(zc, v2f, acc1, fin_add(xe, y_out))
    on_core(1, "z.z1")
    with scope("ahalo"):
        widen_local(ae, ac)
        recv_rows(3, ae)
        widen_rows(ae, ac)
    with scope("ct1own"):
        conv_own(ac, w1t, acc2)
    on_core(0, "BA.p2")
    on_core(1, "Y.z3", "ba.p1m")
    with scope("aplanes"):
        recv_planes(3, ae)
        widen_planes(ae, ac)
    on_core(1, "z.z2")
    with scope("ct1rest"):
        conv_rest(ac, v1t, acc2, fin_add(ge, dx_out))
    on_core(0, "BA.p3", "BA.g3", "BA.g2", "BA.g1", "BA.g1m", "BA.gc")
    on_core(1, "Y.p2", "z.z3", "ba.p2", "Y.p3", "z.p2", "ba.p3", "Y.g1", "z.p3", "ba.g3",
            "Y.w1", "z.g1", "ba.g2", "Y.w2", "z.w1", "ba.g1", "Y.w3", "z.w2", "Y.gc", "ba.g1m",
            "z.w3", "z.gc", "ba.gc")
    on_core(0, "Yzba.fin", "AB.end")
    on_core(1, "AB.fin", "Yzba.end")
    with scope("tail"):
        for sem, region in pending:
            drain(sem, region)


def settle(y, dx, dw, *refs):
    rows = top(ROWS)
    copies = [pltpu.make_async_copy(src, dst, refs[4].at[n])
              for n, (src, dst) in enumerate(zip((y, dx, dw.at[0, rows], dw.at[1, rows]), refs[:4]))]
    for c in copies:
        c.start()
    for c in copies:
        c.wait()


def solution(mesh):
    nrow, ndep = mesh.shape['row'], mesh.shape['dep']
    ny = 4 if nrow >= 16 else 2
    nx, nz = ndep // 2, nrow // ny
    vol = P(None, 'dep', 'row', None, None)

    def local_step(x, w1, w2, g):
        ext = (NB, ND + 2, NR + 2, NW, NC)
        wide = (NB, ND + 2, NR + 2, NW, 3 * NC)
        tile = (NB, ND, NR, NW, NC)
        V = pltpu.VMEM
        DMA = pltpu.SemaphoreType.DMA
        flops = 6 * 2 * NB * ND * NR * NW * ROWS * NC
        out = pl.pallas_call(
            functools.partial(kernel, nx, ny, nz),
            out_shape=(V((2048, NC), BF16),) * 2 + (V((2, PADDED * NC, NC), F32),),
            in_specs=[pl.BlockSpec(memory_space=pl.ANY)] * 4,
            out_specs=(pl.BlockSpec(memory_space=V),) * 3,
            scratch_shapes=[V(ext, BF16)] * 4 + [V(wide, BF16)] * 4 + [V((ROWS, NC), BF16)] * 2
            + [V((2 * PLANE, 2 * NC), BF16)] * 4 + [V((2, 4 * TRIPLE, 2 * NC), BF16)] * 4
            + [V((NB, ND, NR * NW, NC), F32)] + [V((NC, 2048), BF16)] * 2
            + [V((4, 256, 256), F32)] * 2
            + [V((2, PADDED * NC, NC), F32)] + [V((SLOTS, OWN[0], NC), F32)] * 2 + [
                V((SLOTS, 6, PIECE[0] // 2, NC), F32), V((SLOTS, 2, 4, PIECE[2], NC), F32),
                V((SLOTS, 3, SUB[0], NC), F32),
                V((SLOTS, 15, 8, NC), F32), V((SLOTS, nz - 1, ZP, NC), F32),
                V((SLOTS, PIECE[0], NC), F32), V((SLOTS, nz * ZP, NC), F32), V((SLOTS, nz * ZP, NC), F32),
                DMA((16,)), DMA((4, 2)), DMA((4, 2)), DMA((SLOTS, 2)), DMA((SLOTS, 2)),
                DMA((SLOTS, 6)), DMA((SLOTS, 20)), pltpu.SemaphoreType.REGULAR((3,))],
            compiler_params=pltpu.CompilerParams(
                collective_id=0, has_side_effects=True, vmem_limit_bytes=58720256),
            cost_estimate=pl.CostEstimate(flops=flops, bytes_accessed=8000000, transcendentals=0),
            name="resblock",
        )(x, w1.reshape(ROWS, NC), w2.reshape(ROWS, NC), g)
        shapes = [jax.ShapeDtypeStruct((n, NC), t) for n, t in ((2048, BF16), (ROWS, F32)) for _ in "ab"]
        y, dx, dw1, dw2 = pl.pallas_call(
            settle,
            out_shape=shapes,
            in_specs=[pl.BlockSpec(memory_space=V)] * 3,
            out_specs=[pl.BlockSpec(memory_space=pl.ANY)] * 4,
            scratch_shapes=[DMA((4,))],
            compiler_params=pltpu.CompilerParams(vmem_limit_bytes=1048576),
            cost_estimate=pl.CostEstimate(flops=0, bytes_accessed=8000000, transcendentals=0),
            name="settle",
        )(*out)
        return y.reshape(tile), dx.reshape(tile), dw1.reshape(w1.shape), dw2.reshape(w2.shape)

    return jax.shard_map(local_step, mesh=mesh, in_specs=(vol, P(), P(), vol),
                         out_specs=(vol, vol, P(), P()), check_vma=False)
```

time: 421 us -> 68.8 us (0.16); the launches traced: 416 us -> 68.7 us
  waiting for transfers between devices: 271 us -> 0 us
  Pallas kernels: 0 us -> 67.9 us
  starting transfers between devices: 47.1 us -> 0 us
  matrix products: 37.4 us -> 0 us
  local copies, waits for them, and re-layouts: 30.6 us -> 0 us
  other arithmetic: 14.7 us -> 0 us
  between operations: 15.1 us -> 0.8 us
    psum x1 -> x0, waiting for transfers between devices: 271 us -> none  [local_step(): dw_conv1 = lax.psum(conv_tile(x_ext, dpre_bf, WGT_DIMS), ('row', 'dep'))]
    pallas_call x0 -> x2, Pallas kernels: none -> 67.9 us  [the longest x1 65.8 us: local_step(): pl.pallas_call(functools.partial(kernel, nx, ny, nz), out_shape=(V((2048,...]
    ppermute x16 -> x0, starting transfers between devices: 47.1 us -> none  [the longest x8 34.2 us: add_halo(): from_below = lax.ppermute(last_face, axis_name, up_pairs)]
    conv_general_dilated x6 -> x0, matrix products: 37.4 us -> none  [conv_tile(): lax.conv_general_dilated(volume, kernel, (1, 1, 1), ((0, 0), (0, 0), (1,...]
    unnamed x34 -> x0, local copies, waits for them, and re-layouts: 13.6 us -> none
    concatenate x14 -> x0, local copies, waits for them, and re-layouts: 10.7 us -> none  [add_halo(): return jnp.concatenate([from_below, tile_vals, from_above], axis=vol_axis)]
    concatenate x5 -> x0, other arithmetic: 7.63 us -> none  [add_halo(): return jnp.concatenate([from_below, tile_vals, from_above], axis=vol_axis)]
    conv_general_dilated x3 -> x0, other arithmetic: 6.08 us -> none  [conv_tile(): lax.conv_general_dilated(volume, kernel, (1, 1, 1), ((0, 0), (0, 0), (1,...]
  transfers between devices with their start and end apart: 17 -> 0, of which waited for: 2 -> 0; matrix products, arithmetic and copies ran while one was open for 14% -> 0% of each run, Pallas kernels for 0% -> 0%
where the time goes in v2:
time: 68.8 us; the launch traced here: 68.7 us
  Pallas kernels  67.9 us (99%)
  between operations  0.8 us (1%)
    pallas_call x1, Pallas kernels, local_step(): pl.pallas_call(functools.partial(kernel, nx, ny, nz), out_shape=(V((2048,...  65.8 us
    pallas_call x1, Pallas kernels, local_step(): pl.pallas_call(settle, out_shape=shapes, in_specs=[pl.BlockSpec(memory_sp...  2.17 us

profile of v2, /device:TPU:1, one launch (start us, length us, event | category | flops | bytes accessed | tf_op | source)
XLA Modules:
  0.0 68.7 jit_solution(18216037249861743015)
XLA Ops:
  0.6 65.8 %resblock.1 = (bf16[2048,128]{1,0:T(8,128)(2,1)S(1)}, bf16[2048,128]{1,0:T(8,128)(2,1)S(1)}, f32[2,3584,128]{2,1,0:T(8,128)S(1)}) custom-call(bf16[2,2,16,32,128]{4,3,2,1,0:T(8,128)(2,1)} %x_hbm.1, bf16[3456,128]{1,0:T(8,128)(2,1)} %bitcast.8, bf16[3456,128]{1,0:T(8,128)(2,1)} %bitcast.9, bf16[2,2,16,32,128]{4,3,2,1,0:T(8,128)(2,1)} %g_hbm.1), custom_call_target="tpu_custom_call" | custom-call | flops 10871635968 | bytes 8000000 | tf_op jit(solution)/shard_map/resblock/pallas_call | solution.py:665
  66.4 2.2 %settle.1 = (bf16[2048,128]{1,0:T(8,128)(2,1)}, bf16[2048,128]{1,0:T(8,128)(2,1)}, f32[3456,128]{1,0:T(8,128)}, f32[3456,128]{1,0:T(8,128)}) custom-call(bf16[2048,128]{1,0:T(8,128)(2,1)S(1)} %get-tuple-element.11.y, bf16[2048,128]{1,0:T(8,128)(2,1)S(1)} %get-tuple-element.12.dx, f32[2,3584,128]{2,1,0:T(8,128)S(1)} %get-tuple-element.13.dw), custom_call_target="tpu_custom_call" | custom-call | bytes 8000000 | tf_op jit(solution)/shard_map/settle/pallas_call | solution.py:687

commit v3 on v2

--- a/solution.py
+++ b/solution.py
@@ -14,9 +14,8 @@
 NB, ND, NR, NW, NC = 2, 2, 16, 32, 128
 TAPS = 27
 ROWS = TAPS * NC
-PADDED = TAPS + 1
-FIRST = (0, 10, 20)
-COUNT = (10, 10, 8)
+FIRST = (0, 9, 19)
+COUNT = (9, 10, 8)
 RINGS = (4, 4, 8)
 ZP = 16
 BASE = tuple(t * NC for t in FIRST)
@@ -28,7 +27,7 @@
 PLANE = 9 * NC
 TRIPLE = 3 * NC
 CHUNKS = ((0, 0), (0, 8), (1, 0), (1, 8))
-NEIGH = ((1, 0), (-1, 0), (0, 1), (0, -1), (1, 1), (1, -1), (-1, 1), (-1, -1))
+NEIGH = ((1, 0), (-1, 0), (1, 1), (1, -1), (-1, 1), (-1, -1), (0, 1), (0, -1))
 
 
 def top(n):
@@ -48,7 +47,7 @@
            xe, ge, ze, ae, xc, gc, zc, ac,
            w1r, w2r, w1f, w2f, w1t, w2t, v1f, v2f, v1t, v2t, gp, zt, at,
            acc1, acc2, part, crecv, hsum, r1, rz, r2, r15, r3, s1, s2, t2,
-           in_sem, hs_sem, hr_sem, cs_sem, cr_sem, as_sem, ar_sem, greet_sem):
+           in_sem, hs_sem, hr_sem, cs_sem, cr_sem, as_sem, ar_sem, az_sem, greet_sem):
     row, dep = lax.axis_index("row"), lax.axis_index("dep")
     nrow, ndep = nz * ny, nx * 2
     zi, yi = row // ny, row % ny
@@ -88,7 +87,7 @@
     cw = []
 
     def fetch(src, dst):
-        c = pltpu.make_async_copy(src, dst, in_sem.at[2 + len(cw)])
+        c = pltpu.make_async_copy(src, dst, in_sem.at[2 + len(cw) % 7])
         c.start()
         cw.append(c)
 
@@ -123,7 +122,7 @@
                       0: (inner(NR), inner(NR))}[dr]
             out.append(pltpu.make_async_remote_copy(
                 src_ref=ext.at[:, se, sr], dst_ref=ext.at[:, de, tr],
-                send_sem=hs_sem.at[slot, min(k // 2, 1)], recv_sem=hr_sem.at[slot, min(k // 2, 1)],
+                send_sem=hs_sem.at[slot], recv_sem=hr_sem.at[slot, min(k // 2, 1)],
                 device_id=halo_peer(dr, dd), device_id_type=MESH))
         return out
 
@@ -142,8 +141,7 @@
 
     def start_halo(slot, ext, copies):
         start(copies)
-        sent(hs_sem.at[slot, 0], ext.at[:, top(2), top(2)])
-        sent(hs_sem.at[slot, 1], ext.at[:, top(2)])
+        sent(hs_sem.at[slot], ext.at[:, :, top((2 * NR + 8) // 4)])
 
     def recv_rows(slot, ext):
         drain(hr_sem.at[slot, 0], ext.at[:, top(2), top(2)])
@@ -159,17 +157,12 @@
     greet(0)
     fetch_edge(w1_hbm, v1f)
     soon = len(cw)
-    fetch(w1_hbm, w1r)
-    fetch_own(w2_hbm, w2f)
-    fetch_edge(w2_hbm, v2f)
 
     blank = jnp.zeros((TRIPLE, NC), BF16)
     for edge in (v1f, v2f, v1t, v2t):
         for p in DIRS:
             for r in DIRS:
                 edge[p, pl.ds((1 - r) * PLANE, TRIPLE), lanes[r]] = blank
-    for j in range(2):
-        part[j, pl.ds(ROWS, NC)] = jnp.zeros((NC, NC), F32)
     for c in cw[:3]:
         c.wait()
 
@@ -312,6 +305,9 @@
 
     rings = ((x_peer, xi), (y_peer, yi), (z_peer, zi))
 
+    def arrival(n, i):
+        return (ar_sem if n < 2 else az_sem).at[n % 2, i]
+
     def reducer(n, j, g):
         own, piece, sub, n1 = OWN[g], PIECE[g], SUB[g], RINGS[g]
         half = piece // 2
@@ -320,20 +316,21 @@
         (peer1, me1), (peer2, me2) = rings[g], rings[(1, 0, 0)[g]]
         sides = (peer1(1), peer1(n1 - 1))
         everything = crecv.at[n, top(own)]
-        got2, got3, got15 = r2.at[n], r3.at[n], r15.at[n]
+        got2, got3, got15 = r2.at[n, :, top(sub)], r3.at[n], r15.at[n]
 
         def sems(phase, i):
-            return as_sem.at[n, phase], ar_sem.at[n, i]
+            return as_sem.at[n], arrival(n, i)
 
         def arrived(i, region):
-            drain(ar_sem.at[n, i], region)
+            drain(arrival(n, i), region)
 
         def exchange(phase, i, peers, n, src, dst):
-            start([rcopy(src(k), dst(k), *sems(phase, i), peers(k)) for k in others(n)])
+            far_first = sorted(others(n), key=lambda k: -min(k, n - k))
+            start([rcopy(src(k), dst(k), *sems(phase, i), peers(k)) for k in far_first])
 
         def core_send():
             start([rcopy(part.at[j, pl.ds(base, own)], everything,
-                         cs_sem.at[n, 0], cr_sem.at[n, 0], core_peer)])
+                         cs_sem.at[n], cr_sem.at[n, 0], core_peer)])
 
         def rows_of(k, h):
             return ds8(((me1 + k) % n1) * piece + h * half, half)
@@ -351,7 +348,7 @@
 
         def ring_copy(i):
             k, h = ((2, 0), (2, 1), (1, 1), (3, 0), (1, 0), (3, 1))[i]
-            return rcopy(hsum.at[n, rows_of(k, h)], r1.at[n, i],
+            return rcopy(hsum.at[n, rows_of(k, h)], r1.at[n, i, top(half)],
                          *sems(0, min(i, 2)), sides[i % 2])
 
         def p1():
@@ -360,8 +357,8 @@
 
         def p1m():
             for i, k in enumerate((1, 3)):
-                arrived(i, r1.at[n, i])
-                absorb(rows_of(k, i), r1[n, i])
+                arrived(i, r1.at[n, i, top(half)])
+                absorb(rows_of(k, i), r1[n, i, top(half)])
                 start([ring_copy(4 + i)])
 
         def flow(d, s):
@@ -397,13 +394,9 @@
             return step
 
         def plane(phase, i, src, dst):
-            for kx in range(4):
-                for ky in range(4):
-                    k = 4 * kx + ky
-                    if k:
-                        px, py = (xi + kx) % nx, (yi + ky) % nx
-                        start([rcopy(src(px * 4 + py), dst(k - 1), *sems(phase, i),
-                                     (zi * ny + py, px * 2 + ci))])
+            for k in sorted(others(16), key=lambda k: -sum(min(q, nx - q) for q in divmod(k, nx))):
+                px, py = (xi + k // nx) % nx, (yi + k % nx) % nx
+                start([rcopy(src(px * 4 + py), dst(k - 1), *sems(phase, i), (zi * ny + py, px * 2 + ci))])
 
         def z_end():
             for d in DIRS:
@@ -423,17 +416,17 @@
             dw_out[j, rows] = tot
 
         def p2():
-            arrived(2, r1.at[n, pl.ds(2, 4)])
+            arrived(2, r1.at[n, pl.ds(2, 4), top(half)])
             for h, (u, v) in enumerate(((3, 4), (2, 5))):
-                s1[n, part_of(h)] = hsum[n, rows_of(0, h)] + r1[n, u] + r1[n, v]
+                s1[n, part_of(h)] = hsum[n, rows_of(0, h)] + r1[n, u, top(half)] + r1[n, v, top(half)]
             exchange(1, 8, peer2, 4, lambda k: s1.at[n, ds8(((me2 + k) % nx) * sub, sub)],
-                     lambda k: r2.at[n, k - 1])
+                     lambda k: r2.at[n, k - 1, top(sub)])
 
         def p3():
             arrived(8, got2)
             tot = s1[n, ds8(me2 * sub, sub)]
             for k in range(3):
-                tot = tot + r2[n, k]
+                tot = tot + r2[n, k, top(sub)]
             s2[n, top(sub)] = tot
             s2[n, pl.ds(sub, nz * ZP - sub)] = jnp.zeros((nz * ZP - sub, NC), F32)
             exchange(2, 9, z_peer, nz, lambda k: s2.at[n, ds8(((zi + k) % nz) * ZP, ZP)],
@@ -455,7 +448,7 @@
             start([rcopy(dw_mine.at[rows], dw_mine.at[rows], *sems(3 if g == 2 else 5, i), sides[d])])
 
         def to_core(rows):
-            start([rcopy(dw_mine.at[rows], dw_mine.at[rows], cs_sem.at[n, 1], cr_sem.at[n, 1], core_peer)])
+            start([rcopy(dw_mine.at[rows], dw_mine.at[rows], as_sem.at[n], cr_sem.at[n, 1], core_peer)])
 
         def g2():
             arrived(10, got3)
@@ -477,7 +470,7 @@
                 to_core(rows)
 
         def gather_end():
-            arrived(14, r1.at[n, pl.ds(2, 4)])
+            arrived(14, r1.at[n, pl.ds(2, 4), top(half)])
             for k, h in ((3, 1), (1, 0)):
                 to_core(out_rows(k, h, half))
             to_core(out_rows(2))
@@ -504,15 +497,12 @@
             to_core(out_rows(4))
 
         def sent_all():
-            ring_bytes = crecv.at[n, top((n1 - 1) * piece)]
-            middle = (got15, got15) if g == 2 else (got2, got3, got3, got2)
-            for i, region in enumerate((ring_bytes,) + middle + (ring_bytes,)):
-                drain(as_sem.at[n, i], region)
-            drain(cs_sem.at[n, 1], everything)
+            middle = 2 * 15 * 8 if g == 2 else 6 * sub + 2 * (nz - 1) * ZP
+            drain(as_sem.at[n], part.at[:, top((n1 - 1) * piece + (middle + own) // 2)])
 
         def finish():
             drain(cr_sem.at[n, 1], everything)
-            drain(cs_sem.at[n, 0], everything)
+            drain(cs_sem.at[n], everything)
 
         steps = dict(cs=core_send, fin=finish, end=sent_all)
         if g == 2:
@@ -563,12 +553,19 @@
     greet(2)
     for c in cw[3:soon]:
         c.wait()
+    fetch(w1_hbm, w1r)
+    fetch_own(w2_hbm, w2f)
+    fetch_edge(w2_hbm, v2f)
     with scope("xplanes"):
         recv_planes(0, xe)
     with scope("c1rest"):
         widen_planes(xe, xc)
         conv_rest(xc, v1f, acc1, fin_a)
     greet(3)
+    with scope("late"):
+        for c in cw[soon:]:
+            c.wait()
+        flip(w1r, w1t, v1t)
     with scope("gplanes"):
         recv_planes(1, ge)
     with scope("gplanesw"):
@@ -580,58 +577,54 @@
         give(c)
     with scope("ct2rest"):
         conv_rest(gc, v2t, acc2, fin_da)
-    start_halo(3, ae, ha)
     on_core(0, "B.p1")
     on_core(1, "Y.p1")
     with scope("d1z"):
         wgrad(at, xc, 0, 2, False)
     give("z")
     on_core(0, "A.p1")
+    start_halo(3, ae, ha)
     with scope("d1b"):
         wgrad(at, xc, 0, 1, False)
     give("b")
     with scope("d1a"):
         wgrad(at, xc, 0, 0, False)
     give("a")
-    on_core(1, "Y.z1")
-    with scope("late"):
-        for c in cw[soon:]:
-            c.wait()
-        flip(w1r, w1t, v1t)
+    on_core(1, "Y.z1", "z.p1")
     with scope("zhalo"):
         widen_local(ze, zc)
         recv_rows(2, ze)
         widen_rows(ze, zc)
-    on_core(1, "z.p1")
+    on_core(0, "B.p1m")
+    on_core(1, "b.p1")
     with scope("c2own"):
         conv_own(zc, w2f, acc1)
-    on_core(0, "B.p1m", "A.p1m")
-    on_core(1, "b.p1")
+    on_core(1, "a.p1", "z.z1")
     with scope("zplanes"):
         recv_planes(2, ze)
         widen_planes(ze, zc)
-    on_core(1, "a.p1", "Y.z2")
+    on_core(1, "Y.z2")
     with scope("c2rest"):
         conv_rest(zc, v2f, acc1, fin_add(xe, y_out))
-    on_core(1, "z.z1")
+    on_core(0, "A.p1m")
+    on_core(1, "b.p1m")
     with scope("ahalo"):
         widen_local(ae, ac)
         recv_rows(3, ae)
         widen_rows(ae, ac)
+    on_core(0, "B.p2")
     with scope("ct1own"):
         conv_own(ac, w1t, acc2)
-    on_core(0, "BA.p2")
-    on_core(1, "Y.z3", "ba.p1m")
+    on_core(1, "z.z2", "Y.z3", "a.p1m")
     with scope("aplanes"):
         recv_planes(3, ae)
         widen_planes(ae, ac)
-    on_core(1, "z.z2")
     with scope("ct1rest"):
         conv_rest(ac, v1t, acc2, fin_add(ge, dx_out))
-    on_core(0, "BA.p3", "BA.g3", "BA.g2", "BA.g1", "BA.g1m", "BA.gc")
-    on_core(1, "Y.p2", "z.z3", "ba.p2", "Y.p3", "z.p2", "ba.p3", "Y.g1", "z.p3", "ba.g3",
-            "Y.w1", "z.g1", "ba.g2", "Y.w2", "z.w1", "ba.g1", "Y.w3", "z.w2", "Y.gc", "ba.g1m",
-            "z.w3", "z.gc", "ba.gc")
+    on_core(0, "A.p2", "BA.p3", "BA.g3", "BA.g2", "BA.g1", "BA.g1m", "BA.gc")
+    on_core(1, "b.p2", "z.z3", "Y.p2", "a.p2", "b.p3", "z.p2", "Y.p3", "a.p3", "z.p3", "b.g3", "Y.g1",
+            "a.g3", "z.g1", "Y.w1", "b.g2", "a.g2", "z.w1", "Y.w2", "b.g1", "a.g1", "z.w2", "Y.w3",
+            "ba.g1m", "z.w3", "Y.gc", "z.gc", "ba.gc")
     on_core(0, "Yzba.fin", "AB.end")
     on_core(1, "AB.fin", "Yzba.end")
     with scope("tail"):
@@ -664,20 +657,20 @@
         flops = 6 * 2 * NB * ND * NR * NW * ROWS * NC
         out = pl.pallas_call(
             functools.partial(kernel, nx, ny, nz),
-            out_shape=(V((2048, NC), BF16),) * 2 + (V((2, PADDED * NC, NC), F32),),
+            out_shape=(V((2048, NC), BF16),) * 2 + (V((2, ROWS, NC), F32),),
             in_specs=[pl.BlockSpec(memory_space=pl.ANY)] * 4,
             out_specs=(pl.BlockSpec(memory_space=V),) * 3,
             scratch_shapes=[V(ext, BF16)] * 4 + [V(wide, BF16)] * 4 + [V((ROWS, NC), BF16)] * 2
             + [V((2 * PLANE, 2 * NC), BF16)] * 4 + [V((2, 4 * TRIPLE, 2 * NC), BF16)] * 4
             + [V((NB, ND, NR * NW, NC), F32)] + [V((NC, 2048), BF16)] * 2
             + [V((4, 256, 256), F32)] * 2
-            + [V((2, PADDED * NC, NC), F32)] + [V((SLOTS, OWN[0], NC), F32)] * 2 + [
-                V((SLOTS, 6, PIECE[0] // 2, NC), F32), V((SLOTS, 2, 4, PIECE[2], NC), F32),
-                V((SLOTS, 3, SUB[0], NC), F32),
+            + [V((2, ROWS, NC), F32)] + [V((SLOTS, max(OWN), NC), F32)] * 2 + [
+                V((SLOTS, 6, max(PIECE) // 2, NC), F32), V((SLOTS, 2, 4, PIECE[2], NC), F32),
+                V((SLOTS, 3, max(SUB), NC), F32),
                 V((SLOTS, 15, 8, NC), F32), V((SLOTS, nz - 1, ZP, NC), F32),
-                V((SLOTS, PIECE[0], NC), F32), V((SLOTS, nz * ZP, NC), F32), V((SLOTS, nz * ZP, NC), F32),
-                DMA((16,)), DMA((4, 2)), DMA((4, 2)), DMA((SLOTS, 2)), DMA((SLOTS, 2)),
-                DMA((SLOTS, 6)), DMA((SLOTS, 20)), pltpu.SemaphoreType.REGULAR((3,))],
+                V((SLOTS, max(PIECE), NC), F32), V((SLOTS, nz * ZP, NC), F32), V((SLOTS, nz * ZP, NC), F32),
+                DMA((9,)), DMA((4,)), DMA((4, 2)), DMA((SLOTS,)), DMA((SLOTS, 2)),
+                DMA((SLOTS,)), DMA((2, 15)), DMA((2, 20)), pltpu.SemaphoreType.REGULAR((3,))],
             compiler_params=pltpu.CompilerParams(
                 collective_id=0, has_side_effects=True, vmem_limit_bytes=58720256),
             cost_estimate=pl.CostEstimate(flops=flops, bytes_accessed=8000000, transcendentals=0),

time: 68.8 us -> 66.1 us (0.961)
  Pallas kernels: 67.9 us -> 65.2 us
    pallas_call x1, Pallas kernels: 65.8 us -> 63 us  [local_step(): pl.pallas_call(functools.partial(kernel, nx, ny, nz), out_shape=(V((2048,...]
where the time goes in v3:
time: 66.1 us; the launch traced here: 66 us
  Pallas kernels  65.2 us (99%)
  between operations  0.8 us (1%)
    pallas_call x1, Pallas kernels, local_step(): pl.pallas_call(functools.partial(kernel, nx, ny, nz), out_shape=(V((2048,...  63 us
    pallas_call x1, Pallas kernels, local_step(): pl.pallas_call(settle, out_shape=shapes, in_specs=[pl.BlockSpec(memory_sp...  2.17 us

profile of v3, /device:TPU:1, one launch (start us, length us, event | category | flops | bytes accessed | tf_op | source)
XLA Modules:
  0.0 66.0 jit_solution(227927132801048819)
XLA Ops:
  0.6 63.0 %resblock.1 = (bf16[2048,128]{1,0:T(8,128)(2,1)S(1)}, bf16[2048,128]{1,0:T(8,128)(2,1)S(1)}, f32[2,3456,128]{2,1,0:T(8,128)S(1)}) custom-call(bf16[2,2,16,32,128]{4,3,2,1,0:T(8,128)(2,1)} %x_hbm.1, bf16[3456,128]{1,0:T(8,128)(2,1)} %bitcast.8, bf16[3456,128]{1,0:T(8,128)(2,1)} %bitcast.9, bf16[2,2,16,32,128]{4,3,2,1,0:T(8,128)(2,1)} %g_hbm.1), custom_call_target="tpu_custom_call" | custom-call | flops 10871635968 | bytes 8000000 | tf_op jit(solution)/shard_map/resblock/pallas_call | solution.py:658
  63.6 2.2 %settle.1 = (bf16[2048,128]{1,0:T(8,128)(2,1)}, bf16[2048,128]{1,0:T(8,128)(2,1)}, f32[3456,128]{1,0:T(8,128)}, f32[3456,128]{1,0:T(8,128)}) custom-call(bf16[2048,128]{1,0:T(8,128)(2,1)S(1)} %get-tuple-element.11.y, bf16[2048,128]{1,0:T(8,128)(2,1)S(1)} %get-tuple-element.12.dx, f32[2,3456,128]{2,1,0:T(8,128)S(1)} %get-tuple-element.13.dw), custom_call_target="tpu_custom_call" | custom-call | bytes 8000000 | tf_op jit(solution)/shard_map/settle/pallas_call | solution.py:680

commit v4 on v3

--- a/solution.py
+++ b/solution.py
@@ -636,7 +636,7 @@
     rows = top(ROWS)
     copies = [pltpu.make_async_copy(src, dst, refs[4].at[n])
               for n, (src, dst) in enumerate(zip((y, dx, dw.at[0, rows], dw.at[1, rows]), refs[:4]))]
-    for c in copies:
+    for c in reversed(copies):
         c.start()
     for c in copies:
         c.wait()

time: 66.1 us -> 66.1 us (level)
  no operation moved by 1% of the time
where the time goes in v4:
time: 66.1 us; the launch traced here: 66 us
  Pallas kernels  65.2 us (99%)
  between operations  0.8 us (1%)
    pallas_call x1, Pallas kernels, local_step(): pl.pallas_call(functools.partial(kernel, nx, ny, nz), out_shape=(V((2048,...  63 us
    pallas_call x1, Pallas kernels, local_step(): pl.pallas_call(settle, out_shape=shapes, in_specs=[pl.BlockSpec(memory_sp...  2.17 us

profile of v4, /device:TPU:1, one launch (start us, length us, event | category | flops | bytes accessed | tf_op | source)
XLA Modules:
  0.0 66.0 jit_solution(729233474500838110)
XLA Ops:
  0.6 63.0 %resblock.1 = (bf16[2048,128]{1,0:T(8,128)(2,1)S(1)}, bf16[2048,128]{1,0:T(8,128)(2,1)S(1)}, f32[2,3456,128]{2,1,0:T(8,128)S(1)}) custom-call(bf16[2,2,16,32,128]{4,3,2,1,0:T(8,128)(2,1)} %x_hbm.1, bf16[3456,128]{1,0:T(8,128)(2,1)} %bitcast.8, bf16[3456,128]{1,0:T(8,128)(2,1)} %bitcast.9, bf16[2,2,16,32,128]{4,3,2,1,0:T(8,128)(2,1)} %g_hbm.1), custom_call_target="tpu_custom_call" | custom-call | flops 10871635968 | bytes 8000000 | tf_op jit(solution)/shard_map/resblock/pallas_call | solution.py:658
  63.6 2.2 %settle.1 = (bf16[2048,128]{1,0:T(8,128)(2,1)}, bf16[2048,128]{1,0:T(8,128)(2,1)}, f32[3456,128]{1,0:T(8,128)}, f32[3456,128]{1,0:T(8,128)}) custom-call(bf16[2048,128]{1,0:T(8,128)(2,1)S(1)} %get-tuple-element.11.y, bf16[2048,128]{1,0:T(8,128)(2,1)S(1)} %get-tuple-element.12.dx, f32[2,3456,128]{2,1,0:T(8,128)S(1)} %get-tuple-element.13.dw), custom_call_target="tpu_custom_call" | custom-call | bytes 8000000 | tf_op jit(solution)/shard_map/settle/pallas_call | solution.py:680
